TPU v7x, 8 devices: a whole 2x2x1 slice. The times are simulated.
8 devices in a mesh: fld: 1 (over z), col: 2 (over y), row: 4 (over x, core).
Axes of the slice: x: 2, y: 2, z: 1, core: 2. Of those that a mesh axis runs over, the one named last changes fastest.
Arguments:
- u_real: float32 [32, 64, 64, 64], P('fld', None, 'row', 'col')
- u_imag: float32 [32, 64, 64, 64], P('fld', None, 'row', 'col')
- g_filter: float32 [64, 64, 64], P('row', 'col')
Outputs:
- output 1: float32 [32, 64, 64, 64], P('fld', 'row', 'col')
- output 2: float32 [32, 64, 64, 64], P('fld', 'row', 'col')
All inputs are finite; a program needn't handle non-finite values.
Results may differ from a plain program's by a relative error of at most 0.001.
Values are sent between devices in bfloat16 or wider.
A program may use at most 1 GiB of HBM per device.

v0:
```python
import math
import jax
import jax.numpy as jnp
from jax import lax
from jax.sharding import PartitionSpec as P, NamedSharding


def dft_block(length):
    positions = jnp.arange(length)
    phase_steps = (positions[:, None] * positions[None, :]) % length
    angles = phase_steps.astype(jnp.float32) * (2.0 * math.pi / length)
    norm_scale = 1.0 / math.sqrt(length)
    cos_part = jnp.cos(angles) * norm_scale
    sin_part = jnp.sin(angles) * norm_scale
    real_rows = jnp.stack([cos_part, sin_part], axis=1)
    imag_rows = jnp.stack([-sin_part, cos_part], axis=1)
    return jnp.stack([real_rows, imag_rows])


def solution(mesh):
    highest = lax.Precision.HIGHEST

    def local_forward(u_real, u_imag, g_filter):
        dft_mat = dft_block(u_real.shape[1])
        field_pair = jnp.stack([u_real, u_imag])
        field_pair = jnp.einsum("dkcx,cbxyz->dbkyz", dft_mat, field_pair, precision=highest, preferred_element_type=jnp.float32)
        field_pair = lax.all_to_all(field_pair, "row", 2, 3, tiled=True)
        field_pair = jnp.einsum("dkcy,cbxyz->dbxkz", dft_mat, field_pair, precision=highest, preferred_element_type=jnp.float32)
        field_pair = lax.all_to_all(field_pair, "col", 3, 4, tiled=True)
        field_pair = jnp.einsum("dkcz,cbxyz->dbxyk", dft_mat, field_pair, precision=highest, preferred_element_type=jnp.float32)
        filtered = field_pair * g_filter
        return filtered[0], filtered[1]

    field_spec = P("fld", None, "row", "col")
    out_spec = P("fld", "row", "col", None)
    return jax.shard_map(local_forward, mesh=mesh, in_specs=(field_spec, field_spec, P("row", "col", None)), out_specs=(out_spec, out_spec), check_vma=False)
```

profile of v0, /device:TPU:1, one launch (start us, length us, event | category | flops | bytes accessed | tf_op | source)
XLA Modules:
  0.0 776.8 jit_solution(10654007907605281619)
XLA Ops:
  0.6 0.2 sine_multiply_fusion
  0.8 0.1 fusion.20
  1.0 18.6 %fusion.10 = f32[2,32,64,16,32]{2,4,0,3,1:T(8,128)} fusion(f32[1,32,64,16,32]{2,4,0,3,1:T(8,128)} %bitcast.74, f32[1,32,64,16,32]{2,4,0,3,1:T(8,128)} %bitcast.75, f32[1,64,2,64]{3,1,2,0:T(8,128)S(1)} %get-tuple-element.5, f32[1,64,2,64]{3,1,2,0:T(8,128)S(1)} %get-tuple-element.4), kind=kOutput, calls=%fused_computation.11 | convolution fusion | flops 3223339008 | bytes 16842752 | tf_op jit(solution)/shard_map/dkcx,cbxyz->dbkyz/dot_general | solution.py:26
  19.5 42.0 %copy.11 = f32[2,32,64,16,32]{4,0,3,1,2:T(2,128)} copy(f32[2,32,64,16,32]{2,4,0,3,1:T(8,128)} %fusion.10) | data formatting | bytes 16777216 | tf_op jit(solution)/shard_map/dkcx,cbxyz->dbkyz/transpose | solution.py:26
  61.5 38.8 %reshape.94 = f32[4,1,524288]{2,1,0:T(1,128)} reshape(f32[64,32,16,2,32]{4,3,2,1,0:T(2,128)} %bitcast.68) | data formatting | bytes 16777216
  100.3 5.6 all-to-all-start
  105.9 92.4 %all-to-all-done = f32[4,1,524288]{2,1,0:T(1,128)} async-done(((f32[4,1,524288]{2,1,0:T(1,128)}), f32[4,1,524288]{2,1,0:T(1,128)}, u32[]{:S(2)}, u32[]{:S(2)}) %all-to-all-start) | async-done | bytes 8388640 | tf_op jit(solution)/shard_map/all_to_all | solution.py:27
  198.3 0.5 broadcast.141
  198.9 28.9 %reduce = f32[4,524288]{1,0:T(4,128)} reduce(f32[4,1,524288]{2,1,0:T(1,128)} %all-to-all-done, f32[]{:T(128)} %broadcast.141), dimensions={1}, to_apply=%all_to_all.26.reduce_sub_computation | reduce | bytes 16777220 | tf_op jit(solution)/shard_map/all_to_all | solution.py:27
  227.8 62.9 %reshape.95 = f32[64,32,16,2,32]{4,3,2,1,0:T(2,128)} reshape(f32[4,524288]{1,0:T(4,128)} %reduce) | data formatting | bytes 16777216
  290.6 15.0 %copy.12 = f32[2,32,64,16,32]{4,3,2,1,0:T(8,128)S(1)} copy(f32[2,32,64,16,32]{4,0,3,1,2:T(2,128)} %bitcast.70) | data formatting | bytes 16777216 | tf_op jit(solution)/shard_map/all_to_all | solution.py:27
  305.7 13.7 %copy.13 = f32[2,32,16,4,16,32]{5,4,3,2,1,0:T(8,128)} copy(f32[2,32,16,4,16,32]{5,4,2,3,1,0:T(8,128)S(1)} %bitcast.72) | data formatting | bytes 16777216 | tf_op jit(solution)/shard_map/all_to_all | solution.py:27
  319.4 58.2 %fusion.11 = f32[2,32,16,64,32]{3,4,0,2,1:T(8,128)} fusion(f32[2,32,16,64,32,1]{4,3,2,1,0,5:T(8,128)} %bitcast.67, f32[2,64,2,64,1,1]{3,1,2,0,5,4:T(8,128)S(1)} %maximum_bitcast_fusion.12), kind=kOutput, calls=%fused_computation.12 | convolution fusion | flops 3221225472 | bytes 16842752 | tf_op jit(solution)/shard_map/dkcy,cbxyz->dbxkz/dot_general | solution.py:28
  377.7 42.0 %copy.15 = f32[2,32,16,64,32]{4,0,2,1,3:T(2,128)} copy(f32[2,32,16,64,32]{3,4,0,2,1:T(8,128)} %fusion.11) | data formatting | bytes 16777216 | tf_op jit(solution)/shard_map/dkcy,cbxyz->dbxkz/transpose | solution.py:28
  419.6 54.5 %reshape.96 = f32[2,1,1048576]{2,1,0:T(1,128)} reshape(f32[64,32,16,2,32]{4,3,2,1,0:T(2,128)} %bitcast.69) | data formatting | bytes 16777216
  474.2 103.5 %all_to_all.36 = f32[2,1,1048576]{2,1,0:T(1,128)} all-to-all(f32[2,1,1048576]{2,1,0:T(1,128)} %reshape.96), channel_id=1, replica_groups=mesh['fld'=1,'col'=2,'row'=4] {'col'}, dimensions={0} | all-to-all | bytes 16777216 | tf_op jit(solution)/shard_map/all_to_all | solution.py:29
  577.7 31.1 %reduce.1 = f32[2,1048576]{1,0:T(2,128)} reduce(f32[2,1,1048576]{2,1,0:T(1,128)} %all_to_all.36, f32[]{:T(128)} %broadcast.141), dimensions={1}, to_apply=%all_to_all.30.reduce_sub_computation | reduce | bytes 16777220 | tf_op jit(solution)/shard_map/all_to_all | solution.py:29
  608.8 57.4 %reshape.97 = f32[64,32,16,2,32]{4,3,2,1,0:T(2,128)} reshape(f32[2,1048576]{1,0:T(2,128)} %reduce.1) | data formatting | bytes 16777216
  666.4 55.0 %copy.32 = f32[2,32,16,2,32,32]{5,3,4,0,2,1:T(2,128)} copy(f32[2,32,16,2,32,32]{5,0,2,1,4,3:T(2,128)} %bitcast.71) | data formatting | bytes 16777216 | tf_op jit(solution)/shard_map/all_to_all | solution.py:29
  721.4 0.0 copy-start
  721.4 31.4 %reshape.91 = f32[2,32,16,32,64,1]{4,3,0,2,1,5:T(8,128)} reshape(f32[2,32,16,32,2,32]{5,4,3,0,2,1:T(2,128)} %bitcast.73) | data formatting | bytes 16777216 | tf_op jit(solution)/shard_map/all_to_all | solution.py:29
  752.8 0.0 copy-done
  752.8 16.8 %fusion.5 = f32[2,32,16,32,64]{4,3,0,2,1:T(8,128)S(1)} fusion(f32[2,32,16,32,64,1]{4,3,0,2,1,5:T(8,128)} %reshape.91, f32[16,32,64]{2,1,0:T(8,128)S(1)} %copy-done, f32[1,64,2,64]{3,1,2,0:T(8,128)S(1)} %get-tuple-element.5, f32[1,64,2,64]{3,1,2,0:T(8,128)S(1)} %get-tuple-element.4), kind=kOutput, calls=%fused_computation.8 | convolution fusion | flops 3223339008 | bytes 16973824 | tf_op jit(solution)/shard_map/dkcz,cbxyz->dbxyk/dot_general | solution.py:30
  769.7 7.0 slice_bitcast_fusion
  (2 shorter events, 0.0 us)
Async XLA Ops:
  100.3 98.0 %all-to-all-start = ((f32[4,1,524288]{2,1,0:T(1,128)}), f32[4,1,524288]{2,1,0:T(1,128)}, u32[]{:S(2)}, u32[]{:S(2)}) async-start(f32[4,1,524288]{2,1,0:T(1,128)} %reshape.94), calls=%async_computation | async-start | bytes 16777216 | tf_op jit(solution)/shard_map/all_to_all | solution.py:27
  721.4 31.4 %copy-start = (f32[16,32,64]{2,1,0:T(8,128)S(1)}, f32[16,32,64]{2,1,0:T(8,128)}, u32[]{:S(2)}) copy-start(f32[16,32,64]{2,1,0:T(8,128)} %param.5) | copy-start | bytes 393220
where the time goes:
time: 788 us; the launch traced here: 777 us
  local copies, waits for them, and re-layouts  420 us (53%)
  blocking collectives  104 us (13%)
  matrix products  93.6 us (12%)
  waiting for transfers between devices  92.4 us (12%)
  other arithmetic  60.3 us (8%)
    unnamed x6, local copies, waits for them, and re-layouts  214 us
    all_to_all x1, blocking collectives, local_forward(): field_pair = lax.all_to_all(field_pair, 'col', 3, 4, tiled=True)  104 us
    all_to_all x1, waiting for transfers between devices, local_forward(): field_pair = lax.all_to_all(field_pair, 'row', 2, 3, tiled=True)  92.4 us
    all_to_all x2, local copies, waits for them, and re-layouts, local_forward(): field_pair = lax.all_to_all(field_pair, 'col', 3, 4, tiled=True)  86.4 us
    dot_general x1, matrix products, local_forward(): jnp.einsum('dkcy,cbxyz->dbxkz', dft_mat, field_pair, precision=highest, p...  58.2 us
    transpose x1, local copies, waits for them, and re-layouts, local_forward(): jnp.einsum('dkcx,cbxyz->dbkyz', dft_mat, field_pair, precision=highest, p...  42 us
    transpose x1, local copies, waits for them, and re-layouts, local_forward(): jnp.einsum('dkcy,cbxyz->dbxkz', dft_mat, field_pair, precision=highest, p...  42 us
    all_to_all x1, other arithmetic, local_forward(): field_pair = lax.all_to_all(field_pair, 'col', 3, 4, tiled=True)  31.1 us
  transfers between devices with their start and end apart: 1, of which 1 were waited for; matrix products, arithmetic and copies ran while one was open for 0% of the time, Pallas kernels for 0%

commit v1 on v0

v1 whole, which is shorter than its diff:
```python
import functools
import math

import jax
import jax.numpy as jnp
import numpy as np
from jax import lax
from jax.experimental import pallas as pl
from jax.experimental.pallas import tpu as pltpu
from jax.sharding import PartitionSpec as P

MESH = pl.DeviceIdType.MESH
HALF = math.sqrt(0.5)
GROUPS, PACK, UNITS, LAG = 8, 4, 16, 2


def dft4(b):
    (r0, i0), (r1, i1), (r2, i2), (r3, i3) = b
    sr0, si0, sr1, si1 = r0 + r2, i0 + i2, r0 - r2, i0 - i2
    sr2, si2, sr3, si3 = r1 + r3, i1 + i3, r1 - r3, i1 - i3
    return [(sr0 + sr2, si0 + si2), (sr1 + si3, si1 - sr3), (sr0 - sr2, si0 - si2), (sr1 - si3, si1 + sr3)]


def dft8(a):
    even = [(a[j][0] + a[j + 4][0], a[j][1] + a[j + 4][1]) for j in range(4)]
    odd = [(a[j][0] - a[j + 4][0], a[j][1] - a[j + 4][1]) for j in range(4)]
    (r1, i1), (r2, i2), (r3, i3) = odd[1:]
    odd = [odd[0], ((r1 + i1) * HALF, (i1 - r1) * HALF), (i2, -r2), ((i3 - r3) * HALF, (r3 + i3) * -HALF)]
    even, odd = dft4(even), dft4(odd)
    return [(even if k % 2 == 0 else odd)[k // 2] for k in range(8)]


def times(a, tr, ti):
    return a[0] * tr - a[1] * ti, a[0] * ti + a[1] * tr


def twiddle(m):
    angle = -2.0 * math.pi * (m % 64) / 64.0
    return math.cos(angle) / 8.0, math.sin(angle) / 8.0


def lane_matrix():
    z, kz = np.arange(64), np.arange(64)
    angle = 2.0 * np.pi * ((z[:, None] * kz[None, :]) % 64) / 64.0
    cos, sin = np.cos(angle) / 8.0, np.sin(angle) / 8.0
    blocks = np.stack([np.concatenate([cos, -sin], 1), np.concatenate([sin, cos], 1)])
    out = np.zeros((2, 2, PACK, 32, PACK, 128))
    for c in range(2):
        for f in range(PACK):
            out[c, :, f, :, f, :] = blocks[:, 32 * c : 32 * c + 32]
    return out.reshape(2, 256, PACK * 128).astype(np.float32)


def sublane_twiddle():
    k1, x2 = np.arange(8), np.arange(8)
    angle = -2.0 * np.pi * (k1[:, None] * x2[None, :]) / 64.0
    both = np.stack([np.cos(angle), np.sin(angle)]) / 8.0
    return np.broadcast_to(both[..., None], (2, 8, 8, 128)).astype(np.float32)


def kernel(ur, ui, gf, wz, tw, out, inr, ini, xbuf, b2, r2, obuf, wv, tv, gs, gv, asc, bsc, lsc,
           in_sem, c_sem, s1, d1, s2, d2, o_sem):
    row, col = lax.axis_index("row"), lax.axis_index("col")
    core = lax.rem(row, 2)
    dests = [2 - core, 3 - core, 1 + 2 * core]
    other = 1 - col

    barrier = pltpu.get_barrier_semaphore()
    for p in (1, 2, 3):
        pl.semaphore_signal(barrier, inc=1, device_id={"row": lax.rem(row + p, 4)}, device_id_type=MESH)
    pl.semaphore_signal(barrier, inc=1, device_id={"col": other}, device_id_type=MESH)

    def load(g, k):
        src, dst = ((ur, inr), (ui, ini))[k]
        return pltpu.make_async_copy(src.at[g], dst.at[g], in_sem.at[2 * g + k])

    load(0, 0).start()
    load(0, 1).start()
    consts = [
        pltpu.make_async_copy(tw, tv, c_sem.at[0]),
        pltpu.make_async_copy(wz.at[col], wv.at[pl.ds(0, 256)], c_sem.at[1]),
        pltpu.make_async_copy(wz.at[other], wv.at[pl.ds(256, 256)], c_sem.at[2]),
        pltpu.make_async_copy(gf, gs, c_sem.at[3]),
    ]
    consts[0].start()

    @pl.loop(1, GROUPS)
    def _(g):
        load(g, 0).start()
        load(g, 1).start()

    for copy in consts[1:]:
        copy.start()
    consts[0].wait()

    def step_x(g, first, count):
        slots = [3 + lax.rem(k + 4 - row, 4) for k in range(4)]
        bases = [[(2 * g + t) * 7 + slots[k] for t in range(2)] for k in range(4)]

        def one(y, s):
            ar = inr[g, :, y].reshape(PACK * 32, 64).T
            ai = ini[g, :, y].reshape(PACK * 32, 64).T
            a = dft8([(ar[8 * j : 8 * j + 8], ai[8 * j : 8 * j + 8]) for j in range(8)])
            for k1 in range(8):
                vr, vi = times(a[k1], tv[0, k1], tv[1, k1])
                asc[s, 0, pl.ds(8 * k1, 8), :] = vr
                asc[s, 1, pl.ds(8 * k1, 8), :] = vi
            b = dft8([tuple(asc[s, q, pl.ds(x2, 8, stride=8), :] for q in range(2)) for x2 in range(8)])
            for k2 in range(8):
                for q in range(2):
                    xbuf[bases[k2 // 2][k2 % 2], y, q] = b[k2][q]

        @pl.loop(0, count // 2)
        def _(i):
            one(first + 2 * i, 0)
            one(first + 2 * i + 1, 1)

    def send_row(u, j):
        p = dests[j]
        return pltpu.make_async_remote_copy(
            src_ref=xbuf.at[u * 7 + 3 + p], dst_ref=xbuf.at[u * 7 + 3 - p],
            send_sem=s1.at[u * 3 + j], recv_sem=d1.at[u * 3 + 3 - p],
            device_id={"row": lax.rem(row + p, 4)}, device_id_type=MESH)

    def wait_row(u, slot):
        part = xbuf.at[u * 7 + slot]
        pltpu.make_async_remote_copy(
            src_ref=part, dst_ref=part, send_sem=s1.at[u * 3], recv_sem=d1.at[u * 3 + slot],
            device_id={"row": row}, device_id_type=MESH).wait_recv()

    def send_col(u):
        return pltpu.make_async_remote_copy(
            src_ref=b2.at[pl.ds(u * 4 + 2 * other, 2)], dst_ref=r2.at[pl.ds(u * 2, 2)],
            send_sem=s2.at[u], recv_sem=d2.at[u], device_id={"col": other}, device_id_type=MESH)

    def step_y(u):
        slots = [u * 7 + lax.rem(r + 7 - row, 4) for r in range(4)]
        for y2 in range(8):
            a = dft8([tuple(xbuf[slots[y1 // 2], 8 * (y1 % 2) + y2, q] for q in range(2)) for y1 in range(8)])
            for k1 in range(8):
                vr, vi = times(a[k1], *twiddle(k1 * y2))
                bsc[k1, y2, 0] = vr
                bsc[k1, y2, 1] = vi
        for k1 in range(8):
            b = dft8([(bsc[k1, y2, 0], bsc[k1, y2, 1]) for y2 in range(8)])
            for k2 in range(8):
                for q in range(2):
                    b2[u * 4 + 2 * (k2 // 4) + q, pl.ds(8 * (k1 + 8 * (k2 % 4)), 8), :] = b[k2][q]

    def write(u):
        return pltpu.make_async_copy(
            obuf.at[lax.rem(u, 4)],
            out.at[pl.ds(PACK * (u // 2), PACK), pl.ds(8 * lax.rem(u, 2), 8)], o_sem.at[lax.rem(u, 4)])

    def step_z(u):
        for kx in range(8):
            for q in range(2):
                lsc[pl.ds(32 * kx, 32), pl.ds(128 * q, 128)] = b2[u * 4 + 2 * col + q, pl.ds(kx, 32, stride=8), :]
                lsc[pl.ds(32 * kx, 32), pl.ds(256 + 128 * q, 128)] = r2[u * 2 + q, pl.ds(kx, 32, stride=8), :]
        gain = gv[pl.ds(pl.multiple_of(256 * lax.rem(u, 2), 256), 256), :]
        for n in range(2):
            w = jnp.dot(lsc[...], wv[:, 256 * n : 256 * n + 256], precision=lax.Precision.HIGHEST,
                        preferred_element_type=jnp.float32)
            for f in range(2):
                obuf[lax.rem(u, 4), 2 * n + f] = (w[:, 128 * f : 128 * f + 128] * gain).reshape(8, 32, 128)

    for g in range(2):
        load(g, 0).wait()
        load(g, 1).wait()
        step_x(g, 0, 16)
        if g == 0:
            pl.semaphore_wait(barrier, 4)
        for t in range(2):
            for j in range(3):
                send_row(2 * g + t, j).start()

    for copy in consts[1:]:
        copy.wait()
    gain = gs[...].reshape(512, 64)
    gv[...] = jnp.concatenate([gain, gain], axis=1)

    @pl.loop(0, UNITS + LAG)
    def _(t):
        @pl.when(t < UNITS)
        def _():
            for slot in range(3):
                wait_row(t, slot)
            step_y(t)
            send_col(t).start()

        g = t // 2 + 2

        @pl.when(g < GROUPS)
        def _():
            half = lax.rem(t, 2)

            @pl.when(half == 0)
            def _():
                load(g, 0).wait()
                load(g, 1).wait()

            step_x(g, 8 * half, 8)

            @pl.when(half == 1)
            def _():
                for k in range(2):
                    for j in range(3):
                        send_row(2 * g + k, j).start()

        @pl.when(t >= LAG)
        def _():
            u = t - LAG
            send_col(u).wait_recv()

            @pl.when(u >= 4)
            def _():
                write(u - 4).wait()

            step_z(u)
            write(u).start()

    @pl.loop(0, UNITS)
    def _(u):
        for j in range(3):
            send_row(u, j).wait_send()
        send_col(u).wait_send()

    @pl.loop(UNITS - 4, UNITS)
    def _(u):
        write(u).wait()


def solution(mesh):
    f32 = jnp.float32

    def local_forward(u_real, u_imag, g_filter):
        parts = [jnp.transpose(v, (0, 2, 3, 1)).reshape(GROUPS, PACK, 16, 32, 64) for v in (u_real, u_imag)]
        packed = pl.pallas_call(
            kernel,
            out_shape=jax.ShapeDtypeStruct((32, 16, 32, 128), f32),
            in_specs=[pl.BlockSpec(memory_space=pltpu.HBM)] * 5,
            out_specs=pl.BlockSpec(memory_space=pltpu.HBM),
            scratch_shapes=[
                pltpu.VMEM((GROUPS, PACK, 16, 32, 64), f32),
                pltpu.VMEM((GROUPS, PACK, 16, 32, 64), f32),
                pltpu.VMEM((UNITS * 7, 16, 2, 8, 128), f32),
                pltpu.VMEM((UNITS * 4, 256, 128), f32),
                pltpu.VMEM((UNITS * 2, 256, 128), f32),
                pltpu.VMEM((4, PACK, 8, 32, 128), f32),
                pltpu.VMEM((512, 512), f32),
                pltpu.VMEM((2, 8, 8, 128), f32),
                pltpu.VMEM((16, 32, 64), f32),
                pltpu.VMEM((512, 128), f32),
                pltpu.VMEM((2, 2, 64, 128), f32),
                pltpu.VMEM((8, 8, 2, 8, 128), f32),
                pltpu.VMEM((256, 512), f32),
                pltpu.SemaphoreType.DMA((2 * GROUPS,)),
                pltpu.SemaphoreType.DMA((4,)),
                pltpu.SemaphoreType.DMA((3 * UNITS,)),
                pltpu.SemaphoreType.DMA((3 * UNITS,)),
                pltpu.SemaphoreType.DMA((UNITS,)),
                pltpu.SemaphoreType.DMA((UNITS,)),
                pltpu.SemaphoreType.DMA((4,)),
            ],
            compiler_params=pltpu.CompilerParams(
                collective_id=0, has_side_effects=True, vmem_limit_bytes=60 * 1024 * 1024),
            name="dft3",
        )(*parts, g_filter, jnp.asarray(lane_matrix()), jnp.asarray(sublane_twiddle()))
        return packed[..., :64], packed[..., 64:]

    field_spec = P("fld", None, "row", "col")
    out_spec = P("fld", "row", "col", None)
    return jax.shard_map(local_forward, mesh=mesh, in_specs=(field_spec, field_spec, P("row", "col", None)),
                         out_specs=(out_spec, out_spec), check_vma=False)
```

time: 788 us -> 120 us (0.15); the launches traced: 777 us -> 120 us
  local copies, waits for them, and re-layouts: 420 us -> 13 us
  Pallas kernels: 0 us -> 106 us
  blocking collectives: 104 us -> 0 us
  matrix products: 93.6 us -> 0 us
  waiting for transfers between devices: 92.4 us -> 0 us
  other arithmetic: 60.3 us -> 0 us
    unnamed x6 -> x0, local copies, waits for them, and re-layouts: 214 us -> none
    all_to_all x5 -> x0, local copies, waits for them, and re-layouts: 116 us -> none  [the longest x2 86.4 us: local_forward(): field_pair = lax.all_to_all(field_pair, 'col', 3, 4, tiled=True)]
    pallas_call x0 -> x1, Pallas kernels: none -> 106 us  [local_forward(): pl.pallas_call(kernel, out_shape=jax.ShapeDtypeStruct((32, 16, 32, 128),...]
    all_to_all x1 -> x0, blocking collectives: 104 us -> none  [local_forward(): field_pair = lax.all_to_all(field_pair, 'col', 3, 4, tiled=True)]
    dot_general x3 -> x0, matrix products: 93.6 us -> none  [the longest x1 58.2 us: local_forward(): jnp.einsum('dkcy,cbxyz->dbxkz', dft_mat, field_pair, precision=highest, p...]
    all_to_all x1 -> x0, waiting for transfers between devices: 92.4 us -> none  [local_forward(): field_pair = lax.all_to_all(field_pair, 'row', 2, 3, tiled=True)]
    transpose x2 -> x0, local copies, waits for them, and re-layouts: 83.9 us -> none  [the longest x1 42 us: local_forward(): jnp.einsum('dkcx,cbxyz->dbkyz', dft_mat, field_pair, precision=highest, p...]
    all_to_all x2 -> x0, other arithmetic: 60 us -> none  [the longest x1 31.1 us: local_forward(): field_pair = lax.all_to_all(field_pair, 'col', 3, 4, tiled=True)]
  transfers between devices with their start and end apart: 1 -> 0, of which waited for: 1 -> 0; matrix products, arithmetic and copies ran while one was open for 0% -> 0% of each run, Pallas kernels for 0% -> 0%
where the time goes in v1:
time: 120 us
  Pallas kernels  106 us (88%)
  local copies, waits for them, and re-layouts  13 us (11%)
    pallas_call x1, Pallas kernels, local_forward(): pl.pallas_call(kernel, out_shape=jax.ShapeDtypeStruct((32, 16, 32, 128),...  106 us
    slice x1, local copies, waits for them, and re-layouts, local_forward(): return (packed[..., :64], packed[..., 64:])  13 us

profile of v1, /device:TPU:1, one launch (start us, length us, event | category | flops | bytes accessed | tf_op | source)
XLA Modules:
  0.0 119.5 jit_solution(7054106886012085028)
XLA Ops:
  0.6 105.9 %dft3.1 = f32[32,16,32,128]{3,2,1,0:T(8,128)} custom-call(f32[8,4,16,32,64]{4,3,2,1,0:T(8,128)} %bitcast.6, f32[8,4,16,32,64]{4,3,2,1,0:T(8,128)} %bitcast.7, f32[16,32,64]{2,1,0:T(8,128)} %gf.1, f32[2,256,512]{2,1,0:T(8,128)} %constant.4.clone.wz, f32[2,8,8,128]{3,2,1,0:T(8,128)} %constant.5.clone.tw), custom_call_target="tpu_custom_call" | custom-call | tf_op jit(solution)/shard_map/dft3/pallas_call | solution.py:238
  106.5 13.0 %fusion = (f32[32,16,32,64]{3,2,1,0:T(8,128)}, f32[32,16,32,64]{3,2,1,0:T(8,128)}) fusion(f32[32,16,32,128]{3,2,1,0:T(8,128)} %dft3.1), kind=kLoop, calls=%fused_computation | loop fusion | bytes 16777216 | tf_op jit(solution)/shard_map/slice | solution.py:269

commit v2 on v1

--- a/solution.py
+++ b/solution.py
@@ -11,7 +11,7 @@
 
 MESH = pl.DeviceIdType.MESH
 HALF = math.sqrt(0.5)
-GROUPS, PACK, UNITS, LAG = 8, 4, 16, 2
+GROUPS, PACK, UNITS, LAG, RING = 8, 4, 16, 2, 4
 
 
 def dft4(b):
@@ -58,8 +58,8 @@
     return np.broadcast_to(both[..., None], (2, 8, 8, 128)).astype(np.float32)
 
 
-def kernel(ur, ui, gf, wz, tw, out, inr, ini, xbuf, b2, r2, obuf, wv, tv, gs, gv, asc, bsc, lsc,
-           in_sem, c_sem, s1, d1, s2, d2, o_sem):
+def kernel(ur, ui, gf, wz, tw, outr, outi, inr, ini, xbuf, b2, r2, wv, tv, gs, gv, asc, bsc, lsc,
+           in_sem, c_sem, s1, d1, s2, d2):
     row, col = lax.axis_index("row"), lax.axis_index("col")
     core = lax.rem(row, 2)
     dests = [2 - core, 3 - core, 1 + 2 * core]
@@ -72,7 +72,7 @@
 
     def load(g, k):
         src, dst = ((ur, inr), (ui, ini))[k]
-        return pltpu.make_async_copy(src.at[g], dst.at[g], in_sem.at[2 * g + k])
+        return pltpu.make_async_copy(src.at[g], dst.at[lax.rem(g, RING)], in_sem.at[2 * lax.rem(g, RING) + k])
 
     load(0, 0).start()
     load(0, 1).start()
@@ -84,7 +84,7 @@
     ]
     consts[0].start()
 
-    @pl.loop(1, GROUPS)
+    @pl.loop(1, RING)
     def _(g):
         load(g, 0).start()
         load(g, 1).start()
@@ -94,12 +94,13 @@
     consts[0].wait()
 
     def step_x(g, first, count):
+        ring = lax.rem(g, RING)
         slots = [3 + lax.rem(k + 4 - row, 4) for k in range(4)]
         bases = [[(2 * g + t) * 7 + slots[k] for t in range(2)] for k in range(4)]
 
         def one(y, s):
-            ar = inr[g, :, y].reshape(PACK * 32, 64).T
-            ai = ini[g, :, y].reshape(PACK * 32, 64).T
+            ar = inr[ring, :, y].reshape(PACK * 32, 64).T
+            ai = ini[ring, :, y].reshape(PACK * 32, 64).T
             a = dft8([(ar[8 * j : 8 * j + 8], ai[8 * j : 8 * j + 8]) for j in range(8)])
             for k1 in range(8):
                 vr, vi = times(a[k1], tv[0, k1], tv[1, k1])
@@ -115,10 +116,10 @@
             one(first + 2 * i, 0)
             one(first + 2 * i + 1, 1)
 
-    def send_row(u, j):
+    def send_row(u, j, first=0, count=16):
         p = dests[j]
         return pltpu.make_async_remote_copy(
-            src_ref=xbuf.at[u * 7 + 3 + p], dst_ref=xbuf.at[u * 7 + 3 - p],
+            src_ref=xbuf.at[u * 7 + 3 + p, pl.ds(first, count)], dst_ref=xbuf.at[u * 7 + 3 - p, pl.ds(first, count)],
             send_sem=s1.at[u * 3 + j], recv_sem=d1.at[u * 3 + 3 - p],
             device_id={"row": lax.rem(row + p, 4)}, device_id_type=MESH)
 
@@ -147,11 +148,6 @@
                 for q in range(2):
                     b2[u * 4 + 2 * (k2 // 4) + q, pl.ds(8 * (k1 + 8 * (k2 % 4)), 8), :] = b[k2][q]
 
-    def write(u):
-        return pltpu.make_async_copy(
-            obuf.at[lax.rem(u, 4)],
-            out.at[pl.ds(PACK * (u // 2), PACK), pl.ds(8 * lax.rem(u, 2), 8)], o_sem.at[lax.rem(u, 4)])
-
     def step_z(u):
         for kx in range(8):
             for q in range(2):
@@ -162,17 +158,33 @@
             w = jnp.dot(lsc[...], wv[:, 256 * n : 256 * n + 256], precision=lax.Precision.HIGHEST,
                         preferred_element_type=jnp.float32)
             for f in range(2):
-                obuf[lax.rem(u, 4), 2 * n + f] = (w[:, 128 * f : 128 * f + 128] * gain).reshape(8, 32, 128)
-
-    for g in range(2):
-        load(g, 0).wait()
-        load(g, 1).wait()
-        step_x(g, 0, 16)
-        if g == 0:
-            pl.semaphore_wait(barrier, 4)
-        for t in range(2):
-            for j in range(3):
-                send_row(2 * g + t, j).start()
+                pair = w[:, 128 * f : 128 * f + 128] * gain
+                at = (PACK * (u // 2) + 2 * n + f, pl.ds(8 * lax.rem(u, 2), 8))
+                outr[at] = pair[:, :64].reshape(8, 32, 64)
+                outi[at] = pair[:, 64:].reshape(8, 32, 64)
+
+    load(0, 0).wait()
+    load(0, 1).wait()
+    step_x(0, 0, 4)
+    pl.semaphore_wait(barrier, 4)
+    send_row(0, 0, 0, 4).start()
+    send_row(0, 1, 0, 4).start()
+    for y in (4, 8, 12):
+        step_x(0, y, 4)
+        send_row(0, 0, y, 4).start()
+    send_row(0, 1, 4, 12).start()
+    send_row(0, 2).start()
+    for j in range(3):
+        send_row(1, j).start()
+    for k in range(2):
+        load(RING, k).start()
+        load(1, k).wait()
+    step_x(1, 0, 16)
+    for t in range(2):
+        for j in range(3):
+            send_row(2 + t, j).start()
+    for k in range(2):
+        load(RING + 1, k).start()
 
     for copy in consts[1:]:
         copy.wait()
@@ -207,17 +219,16 @@
                     for j in range(3):
                         send_row(2 * g + k, j).start()
 
+                @pl.when(g + RING < GROUPS)
+                def _():
+                    load(g + RING, 0).start()
+                    load(g + RING, 1).start()
+
         @pl.when(t >= LAG)
         def _():
             u = t - LAG
             send_col(u).wait_recv()
-
-            @pl.when(u >= 4)
-            def _():
-                write(u - 4).wait()
-
             step_z(u)
-            write(u).start()
 
     @pl.loop(0, UNITS)
     def _(u):
@@ -225,9 +236,14 @@
             send_row(u, j).wait_send()
         send_col(u).wait_send()
 
-    @pl.loop(UNITS - 4, UNITS)
-    def _(u):
-        write(u).wait()
+
+def put(vr, vi, outr, outi, sem):
+    copies = [pltpu.make_async_copy(v.at[pl.ds(8 * i, 8)], o.at[pl.ds(8 * i, 8)], sem.at[4 * k + i])
+              for i in range(4) for k, (v, o) in enumerate(((vr, outr), (vi, outi)))]
+    for copy in copies:
+        copy.start()
+    for copy in copies:
+        copy.wait()
 
 
 def solution(mesh):
@@ -235,18 +251,17 @@
 
     def local_forward(u_real, u_imag, g_filter):
         parts = [jnp.transpose(v, (0, 2, 3, 1)).reshape(GROUPS, PACK, 16, 32, 64) for v in (u_real, u_imag)]
-        packed = pl.pallas_call(
+        spectrum = pl.pallas_call(
             kernel,
-            out_shape=jax.ShapeDtypeStruct((32, 16, 32, 128), f32),
+            out_shape=[pltpu.VMEM((32, 16, 32, 64), f32)] * 2,
             in_specs=[pl.BlockSpec(memory_space=pltpu.HBM)] * 5,
-            out_specs=pl.BlockSpec(memory_space=pltpu.HBM),
+            out_specs=[pl.BlockSpec(memory_space=pltpu.VMEM)] * 2,
             scratch_shapes=[
-                pltpu.VMEM((GROUPS, PACK, 16, 32, 64), f32),
-                pltpu.VMEM((GROUPS, PACK, 16, 32, 64), f32),
+                pltpu.VMEM((RING, PACK, 16, 32, 64), f32),
+                pltpu.VMEM((RING, PACK, 16, 32, 64), f32),
                 pltpu.VMEM((UNITS * 7, 16, 2, 8, 128), f32),
                 pltpu.VMEM((UNITS * 4, 256, 128), f32),
                 pltpu.VMEM((UNITS * 2, 256, 128), f32),
-                pltpu.VMEM((4, PACK, 8, 32, 128), f32),
                 pltpu.VMEM((512, 512), f32),
                 pltpu.VMEM((2, 8, 8, 128), f32),
                 pltpu.VMEM((16, 32, 64), f32),
@@ -254,19 +269,26 @@
                 pltpu.VMEM((2, 2, 64, 128), f32),
                 pltpu.VMEM((8, 8, 2, 8, 128), f32),
                 pltpu.VMEM((256, 512), f32),
-                pltpu.SemaphoreType.DMA((2 * GROUPS,)),
+                pltpu.SemaphoreType.DMA((2 * RING,)),
                 pltpu.SemaphoreType.DMA((4,)),
                 pltpu.SemaphoreType.DMA((3 * UNITS,)),
                 pltpu.SemaphoreType.DMA((3 * UNITS,)),
                 pltpu.SemaphoreType.DMA((UNITS,)),
                 pltpu.SemaphoreType.DMA((UNITS,)),
-                pltpu.SemaphoreType.DMA((4,)),
             ],
             compiler_params=pltpu.CompilerParams(
-                collective_id=0, has_side_effects=True, vmem_limit_bytes=60 * 1024 * 1024),
+                collective_id=0, has_side_effects=True, vmem_limit_bytes=40 * 1024 * 1024),
             name="dft3",
         )(*parts, g_filter, jnp.asarray(lane_matrix()), jnp.asarray(sublane_twiddle()))
-        return packed[..., :64], packed[..., 64:]
+        return pl.pallas_call(
+            put,
+            out_shape=[jax.ShapeDtypeStruct((32, 16, 32, 64), f32)] * 2,
+            in_specs=[pl.BlockSpec(memory_space=pltpu.VMEM)] * 2,
+            out_specs=[pl.BlockSpec(memory_space=pltpu.HBM)] * 2,
+            scratch_shapes=[pltpu.SemaphoreType.DMA((8,))],
+            compiler_params=pltpu.CompilerParams(vmem_limit_bytes=4 * 1024 * 1024),
+            name="put",
+        )(*spectrum)
 
     field_spec = P("fld", None, "row", "col")
     out_spec = P("fld", "row", "col", None)

time: 120 us -> 112 us (0.933)
  local copies, waits for them, and re-layouts: 13 us -> 0 us
  Pallas kernels: 106 us -> 111 us
    slice x1 -> x0, local copies, waits for them, and re-layouts: 13 us -> none  [local_forward(): return (packed[..., :64], packed[..., 64:])]
    pallas_call x1 -> x2, Pallas kernels: 106 us -> 111 us  [the longest x1 105 us: local_forward(): pl.pallas_call(kernel, out_shape=[pltpu.VMEM((32, 16, 32, 64), f32)] * 2,...]
where the time goes in v2:
time: 112 us
  Pallas kernels  111 us (99%)
    pallas_call x1, Pallas kernels, local_forward(): pl.pallas_call(kernel, out_shape=[pltpu.VMEM((32, 16, 32, 64), f32)] * 2,...  105 us
    pallas_call x1, Pallas kernels, local_forward(): pl.pallas_call(put, out_shape=[jax.ShapeDtypeStruct((32, 16, 32, 64), f32...  5.92 us

profile of v2, /device:TPU:1, one launch (start us, length us, event | category | flops | bytes accessed | tf_op | source)
XLA Modules:
  0.0 111.6 jit_solution(1307681403955779410)
XLA Ops:
  0.6 105.0 %dft3.1 = (f32[32,16,32,64]{3,2,1,0:T(8,128)S(1)}, f32[32,16,32,64]{3,2,1,0:T(8,128)S(1)}) custom-call(f32[8,4,16,32,64]{4,3,2,1,0:T(8,128)} %bitcast.6, f32[8,4,16,32,64]{4,3,2,1,0:T(8,128)} %bitcast.7, f32[16,32,64]{2,1,0:T(8,128)} %gf.1, f32[2,256,512]{2,1,0:T(8,128)} %constant.4.clone.wz, f32[2,8,8,128]{3,2,1,0:T(8,128)} %constant.5.clone.tw), custom_call_target="tpu_custom_call" | custom-call | tf_op jit(solution)/shard_map/dft3/pallas_call | solution.py:254
  105.7 5.9 %put.1 = (f32[32,16,32,64]{3,2,1,0:T(8,128)}, f32[32,16,32,64]{3,2,1,0:T(8,128)}) custom-call(f32[32,16,32,64]{3,2,1,0:T(8,128)S(1)} %get-tuple-element.4.vr, f32[32,16,32,64]{3,2,1,0:T(8,128)S(1)} %get-tuple-element.5.vi), custom_call_target="tpu_custom_call" | custom-call | tf_op jit(solution)/shard_map/put/pallas_call | solution.py:283

commit v3 on v2

--- a/solution.py
+++ b/solution.py
@@ -58,8 +58,18 @@
     return np.broadcast_to(both[..., None], (2, 8, 8, 128)).astype(np.float32)
 
 
-def kernel(ur, ui, gf, wz, tw, outr, outi, inr, ini, xbuf, b2, r2, wv, tv, gs, gv, asc, bsc, lsc,
-           in_sem, c_sem, s1, d1, s2, d2):
+def lane_product(lhs, mat, gain, outr, outi, at):
+    for n in range(2):
+        w = jnp.dot(lhs[...], mat[:, 256 * n : 256 * n + 256], precision=lax.Precision.HIGHEST,
+                    preferred_element_type=jnp.float32)
+        for f in range(2):
+            pair = w[:, 128 * f : 128 * f + 128] * gain
+            outr[at(2 * n + f)] = pair[:, :64].reshape(8, 32, 64)
+            outi[at(2 * n + f)] = pair[:, 64:].reshape(8, 32, 64)
+
+
+def kernel(ur, ui, gf, wz, tw, outr, outi, wv, last, gv, inr, ini, xbuf, b2, r2, tv, gs, asc, bsc, lsc,
+           in_sem, q_sem, c_sem, s1, d1, s2, d2):
     row, col = lax.axis_index("row"), lax.axis_index("col")
     core = lax.rem(row, 2)
     dests = [2 - core, 3 - core, 1 + 2 * core]
@@ -74,24 +84,22 @@
         src, dst = ((ur, inr), (ui, ini))[k]
         return pltpu.make_async_copy(src.at[g], dst.at[lax.rem(g, RING)], in_sem.at[2 * lax.rem(g, RING) + k])
 
-    load(0, 0).start()
-    load(0, 1).start()
+    def quarter(i, k):
+        src, dst = ((ur, inr), (ui, ini))[k]
+        part = (0, slice(None), pl.ds(4 * i, 4))
+        return pltpu.make_async_copy(src.at[part], dst.at[part], q_sem.at[2 * i + k])
+
     consts = [
         pltpu.make_async_copy(tw, tv, c_sem.at[0]),
         pltpu.make_async_copy(wz.at[col], wv.at[pl.ds(0, 256)], c_sem.at[1]),
         pltpu.make_async_copy(wz.at[other], wv.at[pl.ds(256, 256)], c_sem.at[2]),
         pltpu.make_async_copy(gf, gs, c_sem.at[3]),
     ]
-    consts[0].start()
-
-    @pl.loop(1, RING)
-    def _(g):
-        load(g, 0).start()
-        load(g, 1).start()
-
-    for copy in consts[1:]:
-        copy.start()
-    consts[0].wait()
+    for i in range(4):
+        quarter(i, 0).start()
+        quarter(i, 1).start()
+        if i == 0:
+            consts[0].start()
 
     def step_x(g, first, count):
         ring = lax.rem(g, RING)
@@ -148,34 +156,38 @@
                 for q in range(2):
                     b2[u * 4 + 2 * (k2 // 4) + q, pl.ds(8 * (k1 + 8 * (k2 % 4)), 8), :] = b[k2][q]
 
-    def step_z(u):
+    def gather_z(u, dst):
         for kx in range(8):
             for q in range(2):
-                lsc[pl.ds(32 * kx, 32), pl.ds(128 * q, 128)] = b2[u * 4 + 2 * col + q, pl.ds(kx, 32, stride=8), :]
-                lsc[pl.ds(32 * kx, 32), pl.ds(256 + 128 * q, 128)] = r2[u * 2 + q, pl.ds(kx, 32, stride=8), :]
+                dst[pl.ds(32 * kx, 32), pl.ds(128 * q, 128)] = b2[u * 4 + 2 * col + q, pl.ds(kx, 32, stride=8), :]
+                dst[pl.ds(32 * kx, 32), pl.ds(256 + 128 * q, 128)] = r2[u * 2 + q, pl.ds(kx, 32, stride=8), :]
+
+    def step_z(u):
+        gather_z(u, lsc)
         gain = gv[pl.ds(pl.multiple_of(256 * lax.rem(u, 2), 256), 256), :]
-        for n in range(2):
-            w = jnp.dot(lsc[...], wv[:, 256 * n : 256 * n + 256], precision=lax.Precision.HIGHEST,
-                        preferred_element_type=jnp.float32)
-            for f in range(2):
-                pair = w[:, 128 * f : 128 * f + 128] * gain
-                at = (PACK * (u // 2) + 2 * n + f, pl.ds(8 * lax.rem(u, 2), 8))
-                outr[at] = pair[:, :64].reshape(8, 32, 64)
-                outi[at] = pair[:, 64:].reshape(8, 32, 64)
-
-    load(0, 0).wait()
-    load(0, 1).wait()
-    step_x(0, 0, 4)
-    pl.semaphore_wait(barrier, 4)
-    send_row(0, 0, 0, 4).start()
-    send_row(0, 1, 0, 4).start()
-    for y in (4, 8, 12):
-        step_x(0, y, 4)
-        send_row(0, 0, y, 4).start()
+        lane_product(lsc, wv, gain, outr, outi, lambda f: (PACK * (u // 2) + f, pl.ds(8 * lax.rem(u, 2), 8)))
+
+    consts[0].wait()
+    for i in range(4):
+        quarter(i, 0).wait()
+        quarter(i, 1).wait()
+        step_x(0, 4 * i, 4)
+        if i == 0:
+            pl.semaphore_wait(barrier, 4)
+            send_row(0, 1, 0, 4).start()
+        send_row(0, 0, 4 * i, 4).start()
     send_row(0, 1, 4, 12).start()
     send_row(0, 2).start()
     for j in range(3):
         send_row(1, j).start()
+
+    @pl.loop(1, RING)
+    def _(g):
+        load(g, 0).start()
+        load(g, 1).start()
+
+    for copy in consts[1:]:
+        copy.start()
     for k in range(2):
         load(RING, k).start()
         load(1, k).wait()
@@ -191,7 +203,7 @@
     gain = gs[...].reshape(512, 64)
     gv[...] = jnp.concatenate([gain, gain], axis=1)
 
-    @pl.loop(0, UNITS + LAG)
+    @pl.loop(0, UNITS + LAG - 1)
     def _(t):
         @pl.when(t < UNITS)
         def _():
@@ -230,6 +242,9 @@
             send_col(u).wait_recv()
             step_z(u)
 
+    send_col(UNITS - 1).wait_recv()
+    gather_z(UNITS - 1, last)
+
     @pl.loop(0, UNITS)
     def _(u):
         for j in range(3):
@@ -237,12 +252,18 @@
         send_col(u).wait_send()
 
 
-def put(vr, vi, outr, outi, sem):
-    copies = [pltpu.make_async_copy(v.at[pl.ds(8 * i, 8)], o.at[pl.ds(8 * i, 8)], sem.at[4 * k + i])
-              for i in range(4) for k, (v, o) in enumerate(((vr, outr), (vi, outi)))]
+def put(vr, vi, mat, last, gain, outr, outi, lr, li, sem):
+    cuts = [(pl.ds(7 * i, 7), slice(None)) for i in range(4)] + [(pl.ds(28, 4), pl.ds(0, 8))]
+    copies = [pltpu.make_async_copy(v.at[cut], o.at[cut], sem.at[2 * i + k])
+              for i, cut in enumerate(cuts) for k, (v, o) in enumerate(((vr, outr), (vi, outi)))]
     for copy in copies:
         copy.start()
-    for copy in copies:
+    lane_product(last, mat, gain[256:, :], lr, li, lambda f: f)
+    cut = (pl.ds(28, 4), pl.ds(8, 8))
+    tail = [pltpu.make_async_copy(v, o.at[cut], sem.at[10 + k]) for k, (v, o) in enumerate(((lr, outr), (li, outi)))]
+    for copy in tail:
+        copy.start()
+    for copy in copies + tail:
         copy.wait()
 
 
@@ -253,23 +274,23 @@
         parts = [jnp.transpose(v, (0, 2, 3, 1)).reshape(GROUPS, PACK, 16, 32, 64) for v in (u_real, u_imag)]
         spectrum = pl.pallas_call(
             kernel,
-            out_shape=[pltpu.VMEM((32, 16, 32, 64), f32)] * 2,
+            out_shape=[pltpu.VMEM((32, 16, 32, 64), f32)] * 2 + [
+                pltpu.VMEM((512, 512), f32), pltpu.VMEM((256, 512), f32), pltpu.VMEM((512, 128), f32)],
             in_specs=[pl.BlockSpec(memory_space=pltpu.HBM)] * 5,
-            out_specs=[pl.BlockSpec(memory_space=pltpu.VMEM)] * 2,
+            out_specs=[pl.BlockSpec(memory_space=pltpu.VMEM)] * 5,
             scratch_shapes=[
                 pltpu.VMEM((RING, PACK, 16, 32, 64), f32),
                 pltpu.VMEM((RING, PACK, 16, 32, 64), f32),
                 pltpu.VMEM((UNITS * 7, 16, 2, 8, 128), f32),
                 pltpu.VMEM((UNITS * 4, 256, 128), f32),
                 pltpu.VMEM((UNITS * 2, 256, 128), f32),
-                pltpu.VMEM((512, 512), f32),
                 pltpu.VMEM((2, 8, 8, 128), f32),
                 pltpu.VMEM((16, 32, 64), f32),
-                pltpu.VMEM((512, 128), f32),
                 pltpu.VMEM((2, 2, 64, 128), f32),
                 pltpu.VMEM((8, 8, 2, 8, 128), f32),
                 pltpu.VMEM((256, 512), f32),
                 pltpu.SemaphoreType.DMA((2 * RING,)),
+                pltpu.SemaphoreType.DMA((8,)),
                 pltpu.SemaphoreType.DMA((4,)),
                 pltpu.SemaphoreType.DMA((3 * UNITS,)),
                 pltpu.SemaphoreType.DMA((3 * UNITS,)),
@@ -283,10 +304,10 @@
         return pl.pallas_call(
             put,
             out_shape=[jax.ShapeDtypeStruct((32, 16, 32, 64), f32)] * 2,
-            in_specs=[pl.BlockSpec(memory_space=pltpu.VMEM)] * 2,
+            in_specs=[pl.BlockSpec(memory_space=pltpu.VMEM)] * 5,
             out_specs=[pl.BlockSpec(memory_space=pltpu.HBM)] * 2,
-            scratch_shapes=[pltpu.SemaphoreType.DMA((8,))],
-            compiler_params=pltpu.CompilerParams(vmem_limit_bytes=4 * 1024 * 1024),
+            scratch_shapes=[pltpu.VMEM((PACK, 8, 32, 64), f32)] * 2 + [pltpu.SemaphoreType.DMA((12,))],
+            compiler_params=pltpu.CompilerParams(vmem_limit_bytes=8 * 1024 * 1024),
             name="put",
         )(*spectrum)
 

time: 112 us -> 111 us (level)
    pallas_call x1, Pallas kernels: 105 us -> 104 us  [local_forward(): pl.pallas_call(kernel, out_shape=[pltpu.VMEM((32, 16, 32, 64), f32)] * 2...]
where the time goes in v3:
time: 111 us; the launch traced here: 110 us
  Pallas kernels  110 us (99%)
    pallas_call x1, Pallas kernels, local_forward(): pl.pallas_call(kernel, out_shape=[pltpu.VMEM((32, 16, 32, 64), f32)] * 2...  104 us
    pallas_call x1, Pallas kernels, local_forward(): pl.pallas_call(put, out_shape=[jax.ShapeDtypeStruct((32, 16, 32, 64), f32...  5.94 us

profile of v3, /device:TPU:1, one launch (start us, length us, event | category | flops | bytes accessed | tf_op | source)
XLA Modules:
  0.0 110.4 jit_solution(16113780787521063898)
XLA Ops:
  0.6 103.8 %dft3.1 = (f32[32,16,32,64]{3,2,1,0:T(8,128)S(1)}, f32[32,16,32,64]{3,2,1,0:T(8,128)S(1)}, f32[512,512]{1,0:T(8,128)S(1)}, f32[256,512]{1,0:T(8,128)S(1)}, f32[512,128]{1,0:T(8,128)S(1)}) custom-call(f32[8,4,16,32,64]{4,3,2,1,0:T(8,128)} %bitcast.6, f32[8,4,16,32,64]{4,3,2,1,0:T(8,128)} %bitcast.7, f32[16,32,64]{2,1,0:T(8,128)} %gf.1, ...), custom_call_target="tpu_custom_call" | custom-call | tf_op jit(solution)/shard_map/dft3/pallas_call | solution.py:275
  104.5 5.9 %put.1 = (f32[32,16,32,64]{3,2,1,0:T(8,128)}, f32[32,16,32,64]{3,2,1,0:T(8,128)}) custom-call(f32[32,16,32,64]{3,2,1,0:T(8,128)S(1)} %get-tuple-element.7.vr, f32[32,16,32,64]{3,2,1,0:T(8,128)S(1)} %get-tuple-element.8.vi, f32[512,512]{1,0:T(8,128)S(1)} %get-tuple-element.9.mat, f32[256,512]{1,0:T(8,128)S(1)} %get-tuple-element.10.last, ...), custom_call_target="tpu_custom_call" | custom-call | tf_op jit(solution)/shard_map/put/pallas_call | solution.py:304

commit v4 on v3

--- a/solution.py
+++ b/solution.py
@@ -72,7 +72,7 @@
            in_sem, q_sem, c_sem, s1, d1, s2, d2):
     row, col = lax.axis_index("row"), lax.axis_index("col")
     core = lax.rem(row, 2)
-    dests = [2 - core, 3 - core, 1 + 2 * core]
+    dests = [1 + 2 * core, 2 - core, 3 - core]
     other = 1 - col
 
     barrier = pltpu.get_barrier_semaphore()
@@ -174,10 +174,10 @@
         step_x(0, 4 * i, 4)
         if i == 0:
             pl.semaphore_wait(barrier, 4)
-            send_row(0, 1, 0, 4).start()
-        send_row(0, 0, 4 * i, 4).start()
-    send_row(0, 1, 4, 12).start()
-    send_row(0, 2).start()
+            send_row(0, 2, 0, 4).start()
+        send_row(0, 1, 4 * i, 4).start()
+    send_row(0, 0).start()
+    send_row(0, 2, 4, 12).start()
     for j in range(3):
         send_row(1, j).start()
 
@@ -242,14 +242,18 @@
             send_col(u).wait_recv()
             step_z(u)
 
-    send_col(UNITS - 1).wait_recv()
-    gather_z(UNITS - 1, last)
-
     @pl.loop(0, UNITS)
     def _(u):
         for j in range(3):
             send_row(u, j).wait_send()
+
+    @pl.loop(0, UNITS - 1)
+    def _(u):
         send_col(u).wait_send()
+
+    send_col(UNITS - 1).wait_recv()
+    gather_z(UNITS - 1, last)
+    send_col(UNITS - 1).wait_send()
 
 
 def put(vr, vi, mat, last, gain, outr, outi, lr, li, sem):

time: 111 us -> 111 us (level)
  no operation moved by 1% of the time
where the time goes in v4:
time: 111 us; the launch traced here: 110 us
  Pallas kernels  110 us (99%)
    pallas_call x1, Pallas kernels, local_forward(): pl.pallas_call(kernel, out_shape=[pltpu.VMEM((32, 16, 32, 64), f32)] * 2...  104 us
    pallas_call x1, Pallas kernels, local_forward(): pl.pallas_call(put, out_shape=[jax.ShapeDtypeStruct((32, 16, 32, 64), f32...  5.94 us

profile of v4, /device:TPU:1, one launch (start us, length us, event | category | flops | bytes accessed | tf_op | source)
XLA Modules:
  0.0 110.3 jit_solution(6686743455554452433)
XLA Ops:
  0.6 103.7 %dft3.1 = (f32[32,16,32,64]{3,2,1,0:T(8,128)S(1)}, f32[32,16,32,64]{3,2,1,0:T(8,128)S(1)}, f32[512,512]{1,0:T(8,128)S(1)}, f32[256,512]{1,0:T(8,128)S(1)}, f32[512,128]{1,0:T(8,128)S(1)}) custom-call(f32[8,4,16,32,64]{4,3,2,1,0:T(8,128)} %bitcast.6, f32[8,4,16,32,64]{4,3,2,1,0:T(8,128)} %bitcast.7, f32[16,32,64]{2,1,0:T(8,128)} %gf.1, ...), custom_call_target="tpu_custom_call" | custom-call | tf_op jit(solution)/shard_map/dft3/pallas_call | solution.py:279
  104.3 5.9 %put.1 = (f32[32,16,32,64]{3,2,1,0:T(8,128)}, f32[32,16,32,64]{3,2,1,0:T(8,128)}) custom-call(f32[32,16,32,64]{3,2,1,0:T(8,128)S(1)} %get-tuple-element.7.vr, f32[32,16,32,64]{3,2,1,0:T(8,128)S(1)} %get-tuple-element.8.vi, f32[512,512]{1,0:T(8,128)S(1)} %get-tuple-element.9.mat, f32[256,512]{1,0:T(8,128)S(1)} %get-tuple-element.10.last, ...), custom_call_target="tpu_custom_call" | custom-call | tf_op jit(solution)/shard_map/put/pallas_call | solution.py:308

commit v5 on v4

--- a/solution.py
+++ b/solution.py
@@ -178,8 +178,6 @@
         send_row(0, 1, 4 * i, 4).start()
     send_row(0, 0).start()
     send_row(0, 2, 4, 12).start()
-    for j in range(3):
-        send_row(1, j).start()
 
     @pl.loop(1, RING)
     def _(g):
@@ -191,10 +189,9 @@
     for k in range(2):
         load(RING, k).start()
         load(1, k).wait()
+    for j in range(3):
+        send_row(1, j).start()
     step_x(1, 0, 16)
-    for t in range(2):
-        for j in range(3):
-            send_row(2 + t, j).start()
     for k in range(2):
         load(RING + 1, k).start()
 
@@ -212,6 +209,11 @@
             step_y(t)
             send_col(t).start()
 
+            @pl.when(t < UNITS - 2)
+            def _():
+                for j in range(3):
+                    send_row(t + 2, j).start()
+
         g = t // 2 + 2
 
         @pl.when(g < GROUPS)
@@ -227,10 +229,6 @@
 
             @pl.when(half == 1)
             def _():
-                for k in range(2):
-                    for j in range(3):
-                        send_row(2 * g + k, j).start()
-
                 @pl.when(g + RING < GROUPS)
                 def _():
                     load(g + RING, 0).start()

time: 111 us -> 111 us (level)
  no operation moved by 1% of the time
where the time goes in v5:
time: 111 us; the launch traced here: 110 us
  Pallas kernels  110 us (99%)
    pallas_call x1, Pallas kernels, local_forward(): pl.pallas_call(kernel, out_shape=[pltpu.VMEM((32, 16, 32, 64), f32)] * 2...  104 us
    pallas_call x1, Pallas kernels, local_forward(): pl.pallas_call(put, out_shape=[jax.ShapeDtypeStruct((32, 16, 32, 64), f32...  5.94 us

profile of v5, /device:TPU:1, one launch (start us, length us, event | category | flops | bytes accessed | tf_op | source)
XLA Modules:
  0.0 110.3 jit_solution(13330133856904582000)
XLA Ops:
  0.6 103.7 %dft3.1 = (f32[32,16,32,64]{3,2,1,0:T(8,128)S(1)}, f32[32,16,32,64]{3,2,1,0:T(8,128)S(1)}, f32[512,512]{1,0:T(8,128)S(1)}, f32[256,512]{1,0:T(8,128)S(1)}, f32[512,128]{1,0:T(8,128)S(1)}) custom-call(f32[8,4,16,32,64]{4,3,2,1,0:T(8,128)} %bitcast.6, f32[8,4,16,32,64]{4,3,2,1,0:T(8,128)} %bitcast.7, f32[16,32,64]{2,1,0:T(8,128)} %gf.1, ...), custom_call_target="tpu_custom_call" | custom-call | tf_op jit(solution)/shard_map/dft3/pallas_call | solution.py:277
  104.3 5.9 %put.1 = (f32[32,16,32,64]{3,2,1,0:T(8,128)}, f32[32,16,32,64]{3,2,1,0:T(8,128)}) custom-call(f32[32,16,32,64]{3,2,1,0:T(8,128)S(1)} %get-tuple-element.7.vr, f32[32,16,32,64]{3,2,1,0:T(8,128)S(1)} %get-tuple-element.8.vi, f32[512,512]{1,0:T(8,128)S(1)} %get-tuple-element.9.mat, f32[256,512]{1,0:T(8,128)S(1)} %get-tuple-element.10.last, ...), custom_call_target="tpu_custom_call" | custom-call | tf_op jit(solution)/shard_map/put/pallas_call | solution.py:306

commit v6 on v4

--- a/solution.py
+++ b/solution.py
@@ -104,7 +104,7 @@
     def step_x(g, first, count):
         ring = lax.rem(g, RING)
         slots = [3 + lax.rem(k + 4 - row, 4) for k in range(4)]
-        bases = [[(2 * g + t) * 7 + slots[k] for t in range(2)] for k in range(4)]
+        bases = [[slots[k] * UNITS + 2 * g + t for t in range(2)] for k in range(4)]
 
         def one(y, s):
             ar = inr[ring, :, y].reshape(PACK * 32, 64).T
@@ -124,18 +124,29 @@
             one(first + 2 * i, 0)
             one(first + 2 * i + 1, 1)
 
-    def send_row(u, j, first=0, count=16):
+    def send_row(u, n, j, first=0, count=16):
         p = dests[j]
+        src, dst = (3 + p) * UNITS + u, (3 - p) * UNITS + u
         return pltpu.make_async_remote_copy(
-            src_ref=xbuf.at[u * 7 + 3 + p, pl.ds(first, count)], dst_ref=xbuf.at[u * 7 + 3 - p, pl.ds(first, count)],
+            src_ref=xbuf.at[pl.ds(src, n), pl.ds(first, count)], dst_ref=xbuf.at[pl.ds(dst, n), pl.ds(first, count)],
             send_sem=s1.at[u * 3 + j], recv_sem=d1.at[u * 3 + 3 - p],
             device_id={"row": lax.rem(row + p, 4)}, device_id_type=MESH)
 
-    def wait_row(u, slot):
-        part = xbuf.at[u * 7 + slot]
-        pltpu.make_async_remote_copy(
-            src_ref=part, dst_ref=part, send_sem=s1.at[u * 3], recv_sem=d1.at[u * 3 + slot],
-            device_id={"row": row}, device_id_type=MESH).wait_recv()
+    def wait_row(u, n):
+        for slot in range(3):
+            part = xbuf.at[pl.ds(slot * UNITS + u, n)]
+            pltpu.make_async_remote_copy(
+                src_ref=part, dst_ref=part, send_sem=s1.at[u * 3], recv_sem=d1.at[u * 3 + slot],
+                device_id={"row": row}, device_id_type=MESH).wait_recv()
+
+    def batches(t, single, double):
+        @pl.when((t < 2) | (t >= UNITS - 2))
+        def _():
+            single(t)
+
+        @pl.when((t >= 2) & (t < UNITS - 2) & (lax.rem(t, 2) == 0))
+        def _():
+            double(t)
 
     def send_col(u):
         return pltpu.make_async_remote_copy(
@@ -143,7 +154,7 @@
             send_sem=s2.at[u], recv_sem=d2.at[u], device_id={"col": other}, device_id_type=MESH)
 
     def step_y(u):
-        slots = [u * 7 + lax.rem(r + 7 - row, 4) for r in range(4)]
+        slots = [lax.rem(r + 7 - row, 4) * UNITS + u for r in range(4)]
         for y2 in range(8):
             a = dft8([tuple(xbuf[slots[y1 // 2], 8 * (y1 % 2) + y2, q] for q in range(2)) for y1 in range(8)])
             for k1 in range(8):
@@ -174,12 +185,12 @@
         step_x(0, 4 * i, 4)
         if i == 0:
             pl.semaphore_wait(barrier, 4)
-            send_row(0, 2, 0, 4).start()
-        send_row(0, 1, 4 * i, 4).start()
-    send_row(0, 0).start()
-    send_row(0, 2, 4, 12).start()
+            send_row(0, 1, 2, 0, 4).start()
+        send_row(0, 1, 1, 4 * i, 4).start()
+    send_row(0, 1, 0).start()
+    send_row(0, 1, 2, 4, 12).start()
     for j in range(3):
-        send_row(1, j).start()
+        send_row(1, 1, j).start()
 
     @pl.loop(1, RING)
     def _(g):
@@ -192,9 +203,8 @@
         load(RING, k).start()
         load(1, k).wait()
     step_x(1, 0, 16)
-    for t in range(2):
-        for j in range(3):
-            send_row(2 + t, j).start()
+    for j in range(3):
+        send_row(2, 2, j).start()
     for k in range(2):
         load(RING + 1, k).start()
 
@@ -207,8 +217,7 @@
     def _(t):
         @pl.when(t < UNITS)
         def _():
-            for slot in range(3):
-                wait_row(t, slot)
+            batches(t, lambda u: wait_row(u, 1), lambda u: wait_row(u, 2))
             step_y(t)
             send_col(t).start()
 
@@ -227,9 +236,16 @@
 
             @pl.when(half == 1)
             def _():
-                for k in range(2):
+                @pl.when(g < GROUPS - 1)
+                def _():
                     for j in range(3):
-                        send_row(2 * g + k, j).start()
+                        send_row(2 * g, 2, j).start()
+
+                @pl.when(g == GROUPS - 1)
+                def _():
+                    for u in (UNITS - 2, UNITS - 1):
+                        for j in range(3):
+                            send_row(u, 1, j).start()
 
                 @pl.when(g + RING < GROUPS)
                 def _():
@@ -244,8 +260,11 @@
 
     @pl.loop(0, UNITS)
     def _(u):
-        for j in range(3):
-            send_row(u, j).wait_send()
+        def done(u, n):
+            for j in range(3):
+                send_row(u, n, j).wait_send()
+
+        batches(u, lambda u: done(u, 1), lambda u: done(u, 2))
 
     @pl.loop(0, UNITS - 1)
     def _(u):

time: 111 us -> 112 us (level)
  Pallas kernels: 110 us -> 112 us
    pallas_call x1, Pallas kernels: 104 us -> 106 us  [local_forward(): pl.pallas_call(kernel, out_shape=[pltpu.VMEM((32, 16, 32, 64), f32)] * 2...]
where the time goes in v6:
time: 112 us
  Pallas kernels  112 us (100%)
    pallas_call x1, Pallas kernels, local_forward(): pl.pallas_call(kernel, out_shape=[pltpu.VMEM((32, 16, 32, 64), f32)] * 2...  106 us
    pallas_call x1, Pallas kernels, local_forward(): pl.pallas_call(put, out_shape=[jax.ShapeDtypeStruct((32, 16, 32, 64), f32...  5.94 us

profile of v6, /device:TPU:1, one launch (start us, length us, event | category | flops | bytes accessed | tf_op | source)
XLA Modules:
  0.0 112.4 jit_solution(6668029585886261923)
XLA Ops:
  0.6 105.8 %dft3.1 = (f32[32,16,32,64]{3,2,1,0:T(8,128)S(1)}, f32[32,16,32,64]{3,2,1,0:T(8,128)S(1)}, f32[512,512]{1,0:T(8,128)S(1)}, f32[256,512]{1,0:T(8,128)S(1)}, f32[512,128]{1,0:T(8,128)S(1)}) custom-call(f32[8,4,16,32,64]{4,3,2,1,0:T(8,128)} %bitcast.6, f32[8,4,16,32,64]{4,3,2,1,0:T(8,128)} %bitcast.7, f32[16,32,64]{2,1,0:T(8,128)} %gf.1, ...), custom_call_target="tpu_custom_call" | custom-call | tf_op jit(solution)/shard_map/dft3/pallas_call | solution.py:298
  106.4 5.9 %put.1 = (f32[32,16,32,64]{3,2,1,0:T(8,128)}, f32[32,16,32,64]{3,2,1,0:T(8,128)}) custom-call(f32[32,16,32,64]{3,2,1,0:T(8,128)S(1)} %get-tuple-element.7.vr, f32[32,16,32,64]{3,2,1,0:T(8,128)S(1)} %get-tuple-element.8.vi, f32[512,512]{1,0:T(8,128)S(1)} %get-tuple-element.9.mat, f32[256,512]{1,0:T(8,128)S(1)} %get-tuple-element.10.last, ...), custom_call_target="tpu_custom_call" | custom-call | tf_op jit(solution)/shard_map/put/pallas_call | solution.py:327

commit v7 on v4

--- a/solution.py
+++ b/solution.py
@@ -72,7 +72,7 @@
            in_sem, q_sem, c_sem, s1, d1, s2, d2):
     row, col = lax.axis_index("row"), lax.axis_index("col")
     core = lax.rem(row, 2)
-    dests = [1 + 2 * core, 2 - core, 3 - core]
+    dests = [1 + 2 * core, 3 - core, 2 - core]
     other = 1 - col
 
     barrier = pltpu.get_barrier_semaphore()

time: 111 us -> 111 us (level)
  the two profiles are of different devices: /device:TPU:1 before, /device:TPU:0 now
where the time goes in v7:
time: 111 us
  Pallas kernels  110 us (99%)
    pallas_call x1, Pallas kernels, local_forward(): pl.pallas_call(kernel, out_shape=[pltpu.VMEM((32, 16, 32, 64), f32)] * 2...  104 us
    pallas_call x1, Pallas kernels, local_forward(): pl.pallas_call(put, out_shape=[jax.ShapeDtypeStruct((32, 16, 32, 64), f32...  5.94 us

profile of v7, /device:TPU:0, one launch (start us, length us, event | category | flops | bytes accessed | tf_op | source)
XLA Modules:
  0.0 110.7 jit_solution(2303065599362942668)
XLA Ops:
  0.6 104.1 %dft3.1 = (f32[32,16,32,64]{3,2,1,0:T(8,128)S(1)}, f32[32,16,32,64]{3,2,1,0:T(8,128)S(1)}, f32[512,512]{1,0:T(8,128)S(1)}, f32[256,512]{1,0:T(8,128)S(1)}, f32[512,128]{1,0:T(8,128)S(1)}) custom-call(f32[8,4,16,32,64]{4,3,2,1,0:T(8,128)} %bitcast.6, f32[8,4,16,32,64]{4,3,2,1,0:T(8,128)} %bitcast.7, f32[16,32,64]{2,1,0:T(8,128)} %gf.1, ...), custom_call_target="tpu_custom_call" | custom-call | tf_op jit(solution)/shard_map/dft3/pallas_call | solution.py:279
  104.8 5.9 %put.1 = (f32[32,16,32,64]{3,2,1,0:T(8,128)}, f32[32,16,32,64]{3,2,1,0:T(8,128)}) custom-call(f32[32,16,32,64]{3,2,1,0:T(8,128)S(1)} %get-tuple-element.7.vr, f32[32,16,32,64]{3,2,1,0:T(8,128)S(1)} %get-tuple-element.8.vi, f32[512,512]{1,0:T(8,128)S(1)} %get-tuple-element.9.mat, f32[256,512]{1,0:T(8,128)S(1)} %get-tuple-element.10.last, ...), custom_call_target="tpu_custom_call" | custom-call | tf_op jit(solution)/shard_map/put/pallas_call | solution.py:308

commit v8 on v4

--- a/solution.py
+++ b/solution.py
@@ -188,21 +188,6 @@
 
     for copy in consts[1:]:
         copy.start()
-    for k in range(2):
-        load(RING, k).start()
-        load(1, k).wait()
-    step_x(1, 0, 16)
-    for t in range(2):
-        for j in range(3):
-            send_row(2 + t, j).start()
-    for k in range(2):
-        load(RING + 1, k).start()
-
-    for copy in consts[1:]:
-        copy.wait()
-    gain = gs[...].reshape(512, 64)
-    gv[...] = jnp.concatenate([gain, gain], axis=1)
-
     @pl.loop(0, UNITS + LAG - 1)
     def _(t):
         @pl.when(t < UNITS)
@@ -212,11 +197,27 @@
             step_y(t)
             send_col(t).start()
 
-        g = t // 2 + 2
-
-        @pl.when(g < GROUPS)
+        @pl.when(t == 0)
         def _():
-            half = lax.rem(t, 2)
+            for k in range(2):
+                load(RING, k).start()
+                load(1, k).wait()
+            step_x(1, 0, 16)
+            for u in (2, 3):
+                for j in range(3):
+                    send_row(u, j).start()
+            for k in range(2):
+                load(RING + 1, k).start()
+            for copy in consts[1:]:
+                copy.wait()
+            gain = gs[...].reshape(512, 64)
+            gv[...] = jnp.concatenate([gain, gain], axis=1)
+
+        g = (t + 3) // 2
+
+        @pl.when((t >= 1) & (g < GROUPS))
+        def _():
+            half = lax.rem(t + 1, 2)
 
             @pl.when(half == 0)
             def _():

time: 111 us -> 111 us (level)
  no operation moved by 1% of the time
where the time goes in v8:
time: 111 us; the launch traced here: 110 us
  Pallas kernels  110 us (99%)
    pallas_call x1, Pallas kernels, local_forward(): pl.pallas_call(kernel, out_shape=[pltpu.VMEM((32, 16, 32, 64), f32)] * 2...  104 us
    pallas_call x1, Pallas kernels, local_forward(): pl.pallas_call(put, out_shape=[jax.ShapeDtypeStruct((32, 16, 32, 64), f32...  5.94 us

profile of v8, /device:TPU:1, one launch (start us, length us, event | category | flops | bytes accessed | tf_op | source)
XLA Modules:
  0.0 110.3 jit_solution(7808213675067849369)
XLA Ops:
  0.6 103.7 %dft3.1 = (f32[32,16,32,64]{3,2,1,0:T(8,128)S(1)}, f32[32,16,32,64]{3,2,1,0:T(8,128)S(1)}, f32[512,512]{1,0:T(8,128)S(1)}, f32[256,512]{1,0:T(8,128)S(1)}, f32[512,128]{1,0:T(8,128)S(1)}) custom-call(f32[8,4,16,32,64]{4,3,2,1,0:T(8,128)} %bitcast.6, f32[8,4,16,32,64]{4,3,2,1,0:T(8,128)} %bitcast.7, f32[16,32,64]{2,1,0:T(8,128)} %gf.1, ...), custom_call_target="tpu_custom_call" | custom-call | tf_op jit(solution)/shard_map/dft3/pallas_call | solution.py:280
  104.3 5.9 %put.1 = (f32[32,16,32,64]{3,2,1,0:T(8,128)}, f32[32,16,32,64]{3,2,1,0:T(8,128)}) custom-call(f32[32,16,32,64]{3,2,1,0:T(8,128)S(1)} %get-tuple-element.7.vr, f32[32,16,32,64]{3,2,1,0:T(8,128)S(1)} %get-tuple-element.8.vi, f32[512,512]{1,0:T(8,128)S(1)} %get-tuple-element.9.mat, f32[256,512]{1,0:T(8,128)S(1)} %get-tuple-element.10.last, ...), custom_call_target="tpu_custom_call" | custom-call | tf_op jit(solution)/shard_map/put/pallas_call | solution.py:309

commit v9 on v8

--- a/solution.py
+++ b/solution.py
@@ -84,9 +84,11 @@
         src, dst = ((ur, inr), (ui, ini))[k]
         return pltpu.make_async_copy(src.at[g], dst.at[lax.rem(g, RING)], in_sem.at[2 * lax.rem(g, RING) + k])
 
-    def quarter(i, k):
+    pieces = ((0, 2), (2, 2), (4, 4), (8, 8))
+
+    def piece(i, k):
         src, dst = ((ur, inr), (ui, ini))[k]
-        part = (0, slice(None), pl.ds(4 * i, 4))
+        part = (0, slice(None), pl.ds(*pieces[i]))
         return pltpu.make_async_copy(src.at[part], dst.at[part], q_sem.at[2 * i + k])
 
     consts = [
@@ -96,8 +98,8 @@
         pltpu.make_async_copy(gf, gs, c_sem.at[3]),
     ]
     for i in range(4):
-        quarter(i, 0).start()
-        quarter(i, 1).start()
+        piece(i, 0).start()
+        piece(i, 1).start()
         if i == 0:
             consts[0].start()
 
@@ -168,16 +170,15 @@
         lane_product(lsc, wv, gain, outr, outi, lambda f: (PACK * (u // 2) + f, pl.ds(8 * lax.rem(u, 2), 8)))
 
     consts[0].wait()
-    for i in range(4):
-        quarter(i, 0).wait()
-        quarter(i, 1).wait()
-        step_x(0, 4 * i, 4)
+    for i, (first, count) in enumerate(pieces):
+        piece(i, 0).wait()
+        piece(i, 1).wait()
+        step_x(0, first, count)
         if i == 0:
             pl.semaphore_wait(barrier, 4)
-            send_row(0, 2, 0, 4).start()
-        send_row(0, 1, 4 * i, 4).start()
+        send_row(0, 1, first, count).start()
     send_row(0, 0).start()
-    send_row(0, 2, 4, 12).start()
+    send_row(0, 2).start()
     for j in range(3):
         send_row(1, j).start()
 

time: 111 us -> 109 us (0.982)
  no operation moved by 1% of the time
where the time goes in v9:
time: 109 us
  Pallas kernels  109 us (100%)
    pallas_call x1, Pallas kernels, local_forward(): pl.pallas_call(kernel, out_shape=[pltpu.VMEM((32, 16, 32, 64), f32)] * 2...  103 us
    pallas_call x1, Pallas kernels, local_forward(): pl.pallas_call(put, out_shape=[jax.ShapeDtypeStruct((32, 16, 32, 64), f32...  5.94 us

profile of v9, /device:TPU:1, one launch (start us, length us, event | category | flops | bytes accessed | tf_op | source)
XLA Modules:
  0.0 109.2 jit_solution(8026687710139748542)
XLA Ops:
  0.6 102.6 %dft3.1 = (f32[32,16,32,64]{3,2,1,0:T(8,128)S(1)}, f32[32,16,32,64]{3,2,1,0:T(8,128)S(1)}, f32[512,512]{1,0:T(8,128)S(1)}, f32[256,512]{1,0:T(8,128)S(1)}, f32[512,128]{1,0:T(8,128)S(1)}) custom-call(f32[8,4,16,32,64]{4,3,2,1,0:T(8,128)} %bitcast.6, f32[8,4,16,32,64]{4,3,2,1,0:T(8,128)} %bitcast.7, f32[16,32,64]{2,1,0:T(8,128)} %gf.1, ...), custom_call_target="tpu_custom_call" | custom-call | tf_op jit(solution)/shard_map/dft3/pallas_call | solution.py:281
  103.2 5.9 %put.1 = (f32[32,16,32,64]{3,2,1,0:T(8,128)}, f32[32,16,32,64]{3,2,1,0:T(8,128)}) custom-call(f32[32,16,32,64]{3,2,1,0:T(8,128)S(1)} %get-tuple-element.7.vr, f32[32,16,32,64]{3,2,1,0:T(8,128)S(1)} %get-tuple-element.8.vi, f32[512,512]{1,0:T(8,128)S(1)} %get-tuple-element.9.mat, f32[256,512]{1,0:T(8,128)S(1)} %get-tuple-element.10.last, ...), custom_call_target="tpu_custom_call" | custom-call | tf_op jit(solution)/shard_map/put/pallas_call | solution.py:310

commit v10 on v3

--- a/solution.py
+++ b/solution.py
@@ -14,6 +14,10 @@
 GROUPS, PACK, UNITS, LAG, RING = 8, 4, 16, 2, 4
 
 
+def interleave(even, odd):
+    return [v for pair in zip(even, odd) for v in pair]
+
+
 def dft4(b):
     (r0, i0), (r1, i1), (r2, i2), (r3, i3) = b
     sr0, si0, sr1, si1 = r0 + r2, i0 + i2, r0 - r2, i0 - i2
@@ -22,12 +26,32 @@
 
 
 def dft8(a):
-    even = [(a[j][0] + a[j + 4][0], a[j][1] + a[j + 4][1]) for j in range(4)]
-    odd = [(a[j][0] - a[j + 4][0], a[j][1] - a[j + 4][1]) for j in range(4)]
-    (r1, i1), (r2, i2), (r3, i3) = odd[1:]
-    odd = [odd[0], ((r1 + i1) * HALF, (i1 - r1) * HALF), (i2, -r2), ((i3 - r3) * HALF, (r3 + i3) * -HALF)]
+    pairs = list(zip(a[:4], a[4:]))
+    even = [(vr + wr, vi + wi) for (vr, vi), (wr, wi) in pairs]
+    odd = [(vr - wr, vi - wi) for (vr, vi), (wr, wi) in pairs]
+    o0, (r1, i1), (r2, i2), (r3, i3) = odd
+    odd = [o0, ((r1 + i1) * HALF, (i1 - r1) * HALF), (i2, -r2), ((i3 - r3) * HALF, (r3 + i3) * -HALF)]
     even, odd = dft4(even), dft4(odd)
-    return [(even if k % 2 == 0 else odd)[k // 2] for k in range(8)]
+    return interleave(even, odd)
+
+
+def rotate(v):
+    sign = jnp.where(lax.broadcasted_iota(jnp.int32, v.shape, 0) < 4, 1.0, -1.0)
+    return pltpu.roll(v, 4, 0) * sign
+
+
+def packed_dft4(b):
+    b0, b1, b2, b3 = b
+    s0, s1, s2, s3 = b0 + b2, b0 - b2, b1 + b3, rotate(b1 - b3)
+    return [s0 + s2, s1 + s3, s0 - s2, s1 - s3]
+
+
+def packed_dft8(a):
+    pairs = list(zip(a[:4], a[4:]))
+    even = packed_dft4([v + w for v, w in pairs])
+    o0, o1, o2, o3 = [v - w for v, w in pairs]
+    odd = packed_dft4([o0, (rotate(o1) + o1) * HALF, rotate(o2), (rotate(o3) - o3) * HALF])
+    return interleave(even, odd)
 
 
 def times(a, tr, ti):
@@ -72,7 +96,7 @@
            in_sem, q_sem, c_sem, s1, d1, s2, d2):
     row, col = lax.axis_index("row"), lax.axis_index("col")
     core = lax.rem(row, 2)
-    dests = [2 - core, 3 - core, 1 + 2 * core]
+    dests = [1 + 2 * core, 2 - core, 3 - core]
     other = 1 - col
 
     barrier = pltpu.get_barrier_semaphore()
@@ -84,9 +108,11 @@
         src, dst = ((ur, inr), (ui, ini))[k]
         return pltpu.make_async_copy(src.at[g], dst.at[lax.rem(g, RING)], in_sem.at[2 * lax.rem(g, RING) + k])
 
-    def quarter(i, k):
+    pieces = ((0, 2), (2, 2), (4, 4), (8, 8))
+
+    def piece(i, k):
         src, dst = ((ur, inr), (ui, ini))[k]
-        part = (0, slice(None), pl.ds(4 * i, 4))
+        part = (0, slice(None), pl.ds(*pieces[i]))
         return pltpu.make_async_copy(src.at[part], dst.at[part], q_sem.at[2 * i + k])
 
     consts = [
@@ -96,17 +122,18 @@
         pltpu.make_async_copy(gf, gs, c_sem.at[3]),
     ]
     for i in range(4):
-        quarter(i, 0).start()
-        quarter(i, 1).start()
+        piece(i, 0).start()
+        piece(i, 1).start()
         if i == 0:
             consts[0].start()
 
-    def step_x(g, first, count):
+    def step_x(g, first, count, packed=None):
         ring = lax.rem(g, RING)
         slots = [3 + lax.rem(k + 4 - row, 4) for k in range(4)]
         bases = [[(2 * g + t) * 7 + slots[k] for t in range(2)] for k in range(4)]
 
-        def one(y, s):
+        def one(i, s):
+            y = first + 2 * i + s
             ar = inr[ring, :, y].reshape(PACK * 32, 64).T
             ai = ini[ring, :, y].reshape(PACK * 32, 64).T
             a = dft8([(ar[8 * j : 8 * j + 8], ai[8 * j : 8 * j + 8]) for j in range(8)])
@@ -116,13 +143,19 @@
                 asc[s, 1, pl.ds(8 * k1, 8), :] = vi
             b = dft8([tuple(asc[s, q, pl.ds(x2, 8, stride=8), :] for q in range(2)) for x2 in range(8)])
             for k2 in range(8):
-                for q in range(2):
-                    xbuf[bases[k2 // 2][k2 % 2], y, q] = b[k2][q]
+                at, (vr, vi) = bases[k2 // 2][k2 % 2], b[k2]
+                if k2 % 2 == packed:
+                    top = lax.broadcasted_iota(jnp.int32, vr.shape, 0) < 4
+                    xbuf[at, first // 2 + i, s] = jnp.where(top, vr, pltpu.roll(vi, 4, 0))
+                    xbuf[at, 8 + first // 2 + i, s] = jnp.where(top, pltpu.roll(vr, 4, 0), vi)
+                else:
+                    xbuf[at, y, 0] = vr
+                    xbuf[at, y, 1] = vi
 
         @pl.loop(0, count // 2)
         def _(i):
-            one(first + 2 * i, 0)
-            one(first + 2 * i + 1, 1)
+            one(i, 0)
+            one(i, 1)
 
     def send_row(u, j, first=0, count=16):
         p = dests[j]
@@ -141,6 +174,39 @@
         return pltpu.make_async_remote_copy(
             src_ref=b2.at[pl.ds(u * 4 + 2 * other, 2)], dst_ref=r2.at[pl.ds(u * 2, 2)],
             send_sem=s2.at[u], recv_sem=d2.at[u], device_id={"col": other}, device_id_type=MESH)
+
+    def spare(u, h):
+        return u if h == 0 else UNITS + u // (UNITS - 1)
+
+    def send_half(u, h, j, first=0, count=16):
+        p, at, rows = dests[j], spare(u, h), pl.ds(8 * h + first // 2, count // 2)
+        return pltpu.make_async_remote_copy(
+            src_ref=xbuf.at[u * 7 + 3 + p, rows], dst_ref=xbuf.at[u * 7 + 3 - p, rows],
+            send_sem=s1.at[at * 3 + j], recv_sem=d1.at[at * 3 + 3 - p],
+            device_id={"row": lax.rem(row + p, 4)}, device_id_type=MESH)
+
+    def send_col_half(u, h):
+        return pltpu.make_async_remote_copy(
+            src_ref=b2.at[u * 4 + 2 * other + h], dst_ref=r2.at[u * 2 + h],
+            send_sem=s2.at[spare(u, h)], recv_sem=d2.at[spare(u, h)], device_id={"col": other}, device_id_type=MESH)
+
+    def step_y_half(u, h):
+        for slot in range(3):
+            part = xbuf.at[u * 7 + slot, pl.ds(8 * h, 8)]
+            pltpu.make_async_remote_copy(
+                src_ref=part, dst_ref=part, send_sem=s1.at[spare(u, h) * 3], recv_sem=d1.at[spare(u, h) * 3 + slot],
+                device_id={"row": row}, device_id_type=MESH).wait_recv()
+        slots = [u * 7 + lax.rem(r + 7 - row, 4) for r in range(4)]
+        for y2 in range(8):
+            a = packed_dft8([xbuf[slots[y1 // 2], 8 * h + 4 * (y1 % 2) + y2 // 2, y2 % 2] for y1 in range(8)])
+            for k1 in range(8):
+                tr, ti = twiddle(k1 * y2)
+                bsc[k1, y2, 0] = a[k1] * tr - rotate(a[k1]) * ti if k1 * y2 else a[k1] * tr
+        for k1 in range(8):
+            b = packed_dft8([bsc[k1, y2, 0] for y2 in range(8)])
+            for k2 in range(8):
+                b2[u * 4 + 2 * (k2 // 4) + h, pl.ds(8 * (k1 + 8 * (k2 % 4)), 8), :] = b[k2]
+        send_col_half(u, h).start()
 
     def step_y(u):
         slots = [u * 7 + lax.rem(r + 7 - row, 4) for r in range(4)]
@@ -156,28 +222,40 @@
                 for q in range(2):
                     b2[u * 4 + 2 * (k2 // 4) + q, pl.ds(8 * (k1 + 8 * (k2 % 4)), 8), :] = b[k2][q]
 
-    def gather_z(u, dst):
-        for kx in range(8):
+    def gather_z(u, dst, split, kxs=range(8)):
+        for kx in kxs:
             for q in range(2):
-                dst[pl.ds(32 * kx, 32), pl.ds(128 * q, 128)] = b2[u * 4 + 2 * col + q, pl.ds(kx, 32, stride=8), :]
-                dst[pl.ds(32 * kx, 32), pl.ds(256 + 128 * q, 128)] = r2[u * 2 + q, pl.ds(kx, 32, stride=8), :]
+                plane, first = (kx // 4, 4 * q + kx % 4) if split else (q, kx)
+                dst[pl.ds(32 * kx, 32), pl.ds(128 * q, 128)] = b2[u * 4 + 2 * col + plane, pl.ds(first, 32, stride=8), :]
+                dst[pl.ds(32 * kx, 32), pl.ds(256 + 128 * q, 128)] = r2[u * 2 + plane, pl.ds(first, 32, stride=8), :]
 
     def step_z(u):
-        gather_z(u, lsc)
+        @pl.when(u == 0)
+        def _():
+            for h in range(2):
+                send_col_half(0, h).wait_recv()
+            gather_z(0, lsc, True)
+
+        @pl.when(u > 0)
+        def _():
+            send_col(u).wait_recv()
+            gather_z(u, lsc, False)
+
         gain = gv[pl.ds(pl.multiple_of(256 * lax.rem(u, 2), 256), 256), :]
         lane_product(lsc, wv, gain, outr, outi, lambda f: (PACK * (u // 2) + f, pl.ds(8 * lax.rem(u, 2), 8)))
 
     consts[0].wait()
-    for i in range(4):
-        quarter(i, 0).wait()
-        quarter(i, 1).wait()
-        step_x(0, 4 * i, 4)
+    for i, (first, count) in enumerate(pieces):
+        piece(i, 0).wait()
+        piece(i, 1).wait()
+        step_x(0, first, count, packed=0)
         if i == 0:
             pl.semaphore_wait(barrier, 4)
-            send_row(0, 1, 0, 4).start()
-        send_row(0, 0, 4 * i, 4).start()
-    send_row(0, 1, 4, 12).start()
-    send_row(0, 2).start()
+        send_half(0, 0, 1, first, count).start()
+    send_half(0, 0, 0).start()
+    send_half(0, 0, 2).start()
+    for j in range(3):
+        send_half(0, 1, j).start()
     for j in range(3):
         send_row(1, j).start()
 
@@ -188,48 +266,70 @@
 
     for copy in consts[1:]:
         copy.start()
+    for h in range(2):
+        step_y_half(0, h)
     for k in range(2):
         load(RING, k).start()
         load(1, k).wait()
     step_x(1, 0, 16)
-    for t in range(2):
+    for u in (2, 3):
         for j in range(3):
-            send_row(2 + t, j).start()
+            send_row(u, j).start()
     for k in range(2):
         load(RING + 1, k).start()
-
     for copy in consts[1:]:
         copy.wait()
     gain = gs[...].reshape(512, 64)
     gv[...] = jnp.concatenate([gain, gain], axis=1)
 
-    @pl.loop(0, UNITS + LAG - 1)
+    @pl.loop(1, UNITS + LAG - 1)
     def _(t):
-        @pl.when(t < UNITS)
+        @pl.when(t < UNITS - 1)
         def _():
             for slot in range(3):
                 wait_row(t, slot)
             step_y(t)
             send_col(t).start()
 
-        g = t // 2 + 2
+        @pl.when(t == UNITS - 1)
+        def _():
+            for h in range(2):
+                step_y_half(UNITS - 1, h)
+
+        g = (t + 3) // 2
 
         @pl.when(g < GROUPS)
         def _():
-            half = lax.rem(t, 2)
+            half = lax.rem(t + 1, 2)
 
             @pl.when(half == 0)
             def _():
                 load(g, 0).wait()
                 load(g, 1).wait()
 
-            step_x(g, 8 * half, 8)
+            @pl.when(g < GROUPS - 1)
+            def _():
+                step_x(g, 8 * half, 8)
+
+            @pl.when(g == GROUPS - 1)
+            def _():
+                step_x(g, 8 * half, 8, packed=1)
 
             @pl.when(half == 1)
             def _():
-                for k in range(2):
+                for j in range(3):
+                    send_row(2 * g, j).start()
+
+                @pl.when(g < GROUPS - 1)
+                def _():
                     for j in range(3):
-                        send_row(2 * g + k, j).start()
+                        send_row(2 * g + 1, j).start()
+
+                @pl.when(g == GROUPS - 1)
+                def _():
+                    for h in range(2):
+                        for j in range(3):
+                            send_half(UNITS - 1, h, j).start()
 
                 @pl.when(g + RING < GROUPS)
                 def _():
@@ -239,17 +339,25 @@
         @pl.when(t >= LAG)
         def _():
             u = t - LAG
-            send_col(u).wait_recv()
             step_z(u)
 
-    send_col(UNITS - 1).wait_recv()
-    gather_z(UNITS - 1, last)
-
-    @pl.loop(0, UNITS)
+    @pl.loop(1, UNITS - 1)
     def _(u):
         for j in range(3):
             send_row(u, j).wait_send()
         send_col(u).wait_send()
+
+    for u in (0, UNITS - 1):
+        for h in range(2):
+            for j in range(3):
+                send_half(u, h, j).wait_send()
+    for h in range(2):
+        send_col_half(0, h).wait_send()
+    for h in range(2):
+        send_col_half(UNITS - 1, h).wait_recv()
+        gather_z(UNITS - 1, last, True, range(4 * h, 4 * h + 4))
+    for h in range(2):
+        send_col_half(UNITS - 1, h).wait_send()
 
 
 def put(vr, vi, mat, last, gain, outr, outi, lr, li, sem):
@@ -292,10 +400,10 @@
                 pltpu.SemaphoreType.DMA((2 * RING,)),
                 pltpu.SemaphoreType.DMA((8,)),
                 pltpu.SemaphoreType.DMA((4,)),
-                pltpu.SemaphoreType.DMA((3 * UNITS,)),
-                pltpu.SemaphoreType.DMA((3 * UNITS,)),
-                pltpu.SemaphoreType.DMA((UNITS,)),
-                pltpu.SemaphoreType.DMA((UNITS,)),
+                pltpu.SemaphoreType.DMA((3 * UNITS + 6,)),
+                pltpu.SemaphoreType.DMA((3 * UNITS + 6,)),
+                pltpu.SemaphoreType.DMA((UNITS + 2,)),
+                pltpu.SemaphoreType.DMA((UNITS + 2,)),
             ],
             compiler_params=pltpu.CompilerParams(
                 collective_id=0, has_side_effects=True, vmem_limit_bytes=40 * 1024 * 1024),

time: 111 us -> 110 us (level)
  no operation moved by 1% of the time
where the time goes in v10:
time: 110 us
  Pallas kernels  109 us (99%)
    pallas_call x1, Pallas kernels, local_forward(): pl.pallas_call(kernel, out_shape=[pltpu.VMEM((32, 16, 32, 64), f32)] * 2...  103 us
    pallas_call x1, Pallas kernels, local_forward(): pl.pallas_call(put, out_shape=[jax.ShapeDtypeStruct((32, 16, 32, 64), f32...  5.94 us

profile of v10, /device:TPU:1, one launch (start us, length us, event | category | flops | bytes accessed | tf_op | source)
XLA Modules:
  0.0 109.9 jit_solution(100791165363956919)
XLA Ops:
  0.6 103.3 %dft3.1 = (f32[32,16,32,64]{3,2,1,0:T(8,128)S(1)}, f32[32,16,32,64]{3,2,1,0:T(8,128)S(1)}, f32[512,512]{1,0:T(8,128)S(1)}, f32[256,512]{1,0:T(8,128)S(1)}, f32[512,128]{1,0:T(8,128)S(1)}) custom-call(f32[8,4,16,32,64]{4,3,2,1,0:T(8,128)} %bitcast.6, f32[8,4,16,32,64]{4,3,2,1,0:T(8,128)} %bitcast.7, f32[16,32,64]{2,1,0:T(8,128)} %gf.1, ...), custom_call_target="tpu_custom_call" | custom-call | tf_op jit(solution)/shard_map/dft3/pallas_call | solution.py:383
  104.0 5.9 %put.1 = (f32[32,16,32,64]{3,2,1,0:T(8,128)}, f32[32,16,32,64]{3,2,1,0:T(8,128)}) custom-call(f32[32,16,32,64]{3,2,1,0:T(8,128)S(1)} %get-tuple-element.7.vr, f32[32,16,32,64]{3,2,1,0:T(8,128)S(1)} %get-tuple-element.8.vi, f32[512,512]{1,0:T(8,128)S(1)} %get-tuple-element.9.mat, f32[256,512]{1,0:T(8,128)S(1)} %get-tuple-element.10.last, ...), custom_call_target="tpu_custom_call" | custom-call | tf_op jit(solution)/shard_map/put/pallas_call | solution.py:412

commit v11 on v5

--- a/solution.py
+++ b/solution.py
@@ -11,7 +11,11 @@
 
 MESH = pl.DeviceIdType.MESH
 HALF = math.sqrt(0.5)
-GROUPS, PACK, UNITS, LAG, RING = 8, 4, 16, 2, 4
+GROUPS, PACK, UNITS, RING = 8, 4, 32, 4
+
+
+def interleave(even, odd):
+    return [v for pair in zip(even, odd) for v in pair]
 
 
 def dft4(b):
@@ -22,12 +26,32 @@
 
 
 def dft8(a):
-    even = [(a[j][0] + a[j + 4][0], a[j][1] + a[j + 4][1]) for j in range(4)]
-    odd = [(a[j][0] - a[j + 4][0], a[j][1] - a[j + 4][1]) for j in range(4)]
-    (r1, i1), (r2, i2), (r3, i3) = odd[1:]
-    odd = [odd[0], ((r1 + i1) * HALF, (i1 - r1) * HALF), (i2, -r2), ((i3 - r3) * HALF, (r3 + i3) * -HALF)]
+    pairs = list(zip(a[:4], a[4:]))
+    even = [(vr + wr, vi + wi) for (vr, vi), (wr, wi) in pairs]
+    odd = [(vr - wr, vi - wi) for (vr, vi), (wr, wi) in pairs]
+    o0, (r1, i1), (r2, i2), (r3, i3) = odd
+    odd = [o0, ((r1 + i1) * HALF, (i1 - r1) * HALF), (i2, -r2), ((i3 - r3) * HALF, (r3 + i3) * -HALF)]
     even, odd = dft4(even), dft4(odd)
-    return [(even if k % 2 == 0 else odd)[k // 2] for k in range(8)]
+    return interleave(even, odd)
+
+
+def rotate(v):
+    sign = jnp.where(lax.broadcasted_iota(jnp.int32, v.shape, 0) < 4, 1.0, -1.0)
+    return pltpu.roll(v, 4, 0) * sign
+
+
+def packed_dft4(b):
+    b0, b1, b2, b3 = b
+    s0, s1, s2, s3 = b0 + b2, b0 - b2, b1 + b3, rotate(b1 - b3)
+    return [s0 + s2, s1 + s3, s0 - s2, s1 - s3]
+
+
+def packed_dft8(a):
+    pairs = list(zip(a[:4], a[4:]))
+    even = packed_dft4([v + w for v, w in pairs])
+    o0, o1, o2, o3 = [v - w for v, w in pairs]
+    odd = packed_dft4([o0, (rotate(o1) + o1) * HALF, rotate(o2), (rotate(o3) - o3) * HALF])
+    return interleave(even, odd)
 
 
 def times(a, tr, ti):
@@ -84,9 +108,11 @@
         src, dst = ((ur, inr), (ui, ini))[k]
         return pltpu.make_async_copy(src.at[g], dst.at[lax.rem(g, RING)], in_sem.at[2 * lax.rem(g, RING) + k])
 
-    def quarter(i, k):
+    pieces = ((0, 2), (2, 2), (4, 4), (8, 8))
+
+    def piece(i, k):
         src, dst = ((ur, inr), (ui, ini))[k]
-        part = (0, slice(None), pl.ds(4 * i, 4))
+        part = (0, slice(None), pl.ds(*pieces[i]))
         return pltpu.make_async_copy(src.at[part], dst.at[part], q_sem.at[2 * i + k])
 
     consts = [
@@ -96,17 +122,17 @@
         pltpu.make_async_copy(gf, gs, c_sem.at[3]),
     ]
     for i in range(4):
-        quarter(i, 0).start()
-        quarter(i, 1).start()
+        piece(i, 0).start()
+        piece(i, 1).start()
         if i == 0:
             consts[0].start()
 
     def step_x(g, first, count):
         ring = lax.rem(g, RING)
-        slots = [3 + lax.rem(k + 4 - row, 4) for k in range(4)]
-        bases = [[(2 * g + t) * 7 + slots[k] for t in range(2)] for k in range(4)]
-
-        def one(y, s):
+        bases = [4 * g * 7 + 3 + lax.rem(k + 4 - row, 4) for k in range(4)]
+
+        def one(i, s):
+            y = first + 2 * i + s
             ar = inr[ring, :, y].reshape(PACK * 32, 64).T
             ai = ini[ring, :, y].reshape(PACK * 32, 64).T
             a = dft8([(ar[8 * j : 8 * j + 8], ai[8 * j : 8 * j + 8]) for j in range(8)])
@@ -115,14 +141,16 @@
                 asc[s, 0, pl.ds(8 * k1, 8), :] = vr
                 asc[s, 1, pl.ds(8 * k1, 8), :] = vi
             b = dft8([tuple(asc[s, q, pl.ds(x2, 8, stride=8), :] for q in range(2)) for x2 in range(8)])
-            for k2 in range(8):
-                for q in range(2):
-                    xbuf[bases[k2 // 2][k2 % 2], y, q] = b[k2][q]
+            top = lax.broadcasted_iota(jnp.int32, (8, 128), 0) < 4
+            for k2, (vr, vi) in enumerate(b):
+                at = bases[k2 // 2] + 14 * (k2 % 2)
+                xbuf[at, y] = jnp.where(top, vr, pltpu.roll(vi, 4, 0))
+                xbuf[at + 7, y] = jnp.where(top, pltpu.roll(vr, 4, 0), vi)
 
         @pl.loop(0, count // 2)
         def _(i):
-            one(first + 2 * i, 0)
-            one(first + 2 * i + 1, 1)
+            one(i, 0)
+            one(i, 1)
 
     def send_row(u, j, first=0, count=16):
         p = dests[j]
@@ -139,45 +167,57 @@
 
     def send_col(u):
         return pltpu.make_async_remote_copy(
-            src_ref=b2.at[pl.ds(u * 4 + 2 * other, 2)], dst_ref=r2.at[pl.ds(u * 2, 2)],
+            src_ref=b2.at[u * 2 + other], dst_ref=r2.at[u],
             send_sem=s2.at[u], recv_sem=d2.at[u], device_id={"col": other}, device_id_type=MESH)
 
     def step_y(u):
+        for slot in range(3):
+            wait_row(u, slot)
         slots = [u * 7 + lax.rem(r + 7 - row, 4) for r in range(4)]
         for y2 in range(8):
-            a = dft8([tuple(xbuf[slots[y1 // 2], 8 * (y1 % 2) + y2, q] for q in range(2)) for y1 in range(8)])
+            a = packed_dft8([xbuf[slots[y1 // 2], 8 * (y1 % 2) + y2] for y1 in range(8)])
             for k1 in range(8):
-                vr, vi = times(a[k1], *twiddle(k1 * y2))
-                bsc[k1, y2, 0] = vr
-                bsc[k1, y2, 1] = vi
+                tr, ti = twiddle(k1 * y2)
+                bsc[k1, y2] = a[k1] * tr - rotate(a[k1]) * ti if k1 * y2 else a[k1] * tr
         for k1 in range(8):
-            b = dft8([(bsc[k1, y2, 0], bsc[k1, y2, 1]) for y2 in range(8)])
+            b = packed_dft8([bsc[k1, y2] for y2 in range(8)])
             for k2 in range(8):
-                for q in range(2):
-                    b2[u * 4 + 2 * (k2 // 4) + q, pl.ds(8 * (k1 + 8 * (k2 % 4)), 8), :] = b[k2][q]
+                b2[u * 2 + k2 // 4, pl.ds(8 * (k1 + 8 * (k2 % 4)), 8), :] = b[k2]
+        send_col(u).start()
 
     def gather_z(u, dst):
+        send_col(u).wait_recv()
+        send_col(u + 1).wait_recv()
         for kx in range(8):
+            v = u + kx // 4
             for q in range(2):
-                dst[pl.ds(32 * kx, 32), pl.ds(128 * q, 128)] = b2[u * 4 + 2 * col + q, pl.ds(kx, 32, stride=8), :]
-                dst[pl.ds(32 * kx, 32), pl.ds(256 + 128 * q, 128)] = r2[u * 2 + q, pl.ds(kx, 32, stride=8), :]
-
-    def step_z(u):
-        gather_z(u, lsc)
-        gain = gv[pl.ds(pl.multiple_of(256 * lax.rem(u, 2), 256), 256), :]
-        lane_product(lsc, wv, gain, outr, outi, lambda f: (PACK * (u // 2) + f, pl.ds(8 * lax.rem(u, 2), 8)))
+                rows = pl.ds(4 * q + kx % 4, 32, stride=8)
+                dst[pl.ds(32 * kx, 32), pl.ds(128 * q, 128)] = b2[v * 2 + col, rows, :]
+                dst[pl.ds(32 * kx, 32), pl.ds(256 + 128 * q, 128)] = r2[v, rows, :]
+
+    def step_z(m):
+        gather_z(2 * m, lsc)
+        gain = gv[pl.ds(pl.multiple_of(256 * lax.rem(m, 2), 256), 256), :]
+        lane_product(lsc, wv, gain, outr, outi, lambda f: (PACK * (m // 2) + f, pl.ds(8 * lax.rem(m, 2), 8)))
 
     consts[0].wait()
-    for i in range(4):
-        quarter(i, 0).wait()
-        quarter(i, 1).wait()
-        step_x(0, 4 * i, 4)
+    for i, (first, count) in enumerate(pieces):
+        piece(i, 0).wait()
+        piece(i, 1).wait()
+        step_x(0, first, count)
         if i == 0:
             pl.semaphore_wait(barrier, 4)
-            send_row(0, 2, 0, 4).start()
-        send_row(0, 1, 4 * i, 4).start()
+        send_row(0, 1, first, count).start()
     send_row(0, 0).start()
-    send_row(0, 2, 4, 12).start()
+    send_row(0, 2).start()
+
+    def send_rows(first, last):
+        @pl.loop(first, last)
+        def _(u):
+            for j in range(3):
+                send_row(u, j).start()
+
+    send_rows(1, 4)
 
     @pl.loop(1, RING)
     def _(g):
@@ -186,71 +226,57 @@
 
     for copy in consts[1:]:
         copy.start()
+    step_y(0)
     for k in range(2):
         load(RING, k).start()
         load(1, k).wait()
-    for j in range(3):
-        send_row(1, j).start()
     step_x(1, 0, 16)
+    send_rows(4, 8)
     for k in range(2):
         load(RING + 1, k).start()
-
     for copy in consts[1:]:
         copy.wait()
     gain = gs[...].reshape(512, 64)
     gv[...] = jnp.concatenate([gain, gain], axis=1)
 
-    @pl.loop(0, UNITS + LAG - 1)
+    @pl.loop(1, UNITS)
     def _(t):
-        @pl.when(t < UNITS)
-        def _():
-            for slot in range(3):
-                wait_row(t, slot)
-            step_y(t)
-            send_col(t).start()
-
-            @pl.when(t < UNITS - 2)
-            def _():
-                for j in range(3):
-                    send_row(t + 2, j).start()
-
-        g = t // 2 + 2
+        step_y(t)
+        g, i = (t + 7) // 4, lax.rem(t + 3, 4)
 
         @pl.when(g < GROUPS)
         def _():
-            half = lax.rem(t, 2)
-
-            @pl.when(half == 0)
+            @pl.when(i == 0)
             def _():
                 load(g, 0).wait()
                 load(g, 1).wait()
 
-            step_x(g, 8 * half, 8)
-
-            @pl.when(half == 1)
+            step_x(g, 4 * i, 4)
+
+            @pl.when(i == 3)
             def _():
+                send_rows(4 * g, 4 * g + 4)
+
                 @pl.when(g + RING < GROUPS)
                 def _():
                     load(g + RING, 0).start()
                     load(g + RING, 1).start()
 
-        @pl.when(t >= LAG)
+        @pl.when((t >= 3) & (lax.rem(t, 2) == 1))
         def _():
-            u = t - LAG
-            send_col(u).wait_recv()
-            step_z(u)
+            step_z((t - 3) // 2)
 
     @pl.loop(0, UNITS)
     def _(u):
         for j in range(3):
             send_row(u, j).wait_send()
 
-    @pl.loop(0, UNITS - 1)
+    @pl.loop(0, UNITS - 2)
     def _(u):
         send_col(u).wait_send()
 
-    send_col(UNITS - 1).wait_recv()
-    gather_z(UNITS - 1, last)
+    gather_z(UNITS - 2, last)
+    send_col(UNITS - 2).wait_send()
     send_col(UNITS - 1).wait_send()
 
 
@@ -283,13 +309,13 @@
             scratch_shapes=[
                 pltpu.VMEM((RING, PACK, 16, 32, 64), f32),
                 pltpu.VMEM((RING, PACK, 16, 32, 64), f32),
-                pltpu.VMEM((UNITS * 7, 16, 2, 8, 128), f32),
-                pltpu.VMEM((UNITS * 4, 256, 128), f32),
+                pltpu.VMEM((UNITS * 7, 16, 8, 128), f32),
                 pltpu.VMEM((UNITS * 2, 256, 128), f32),
+                pltpu.VMEM((UNITS, 256, 128), f32),
                 pltpu.VMEM((2, 8, 8, 128), f32),
                 pltpu.VMEM((16, 32, 64), f32),
                 pltpu.VMEM((2, 2, 64, 128), f32),
-                pltpu.VMEM((8, 8, 2, 8, 128), f32),
+                pltpu.VMEM((8, 8, 8, 128), f32),
                 pltpu.VMEM((256, 512), f32),
                 pltpu.SemaphoreType.DMA((2 * RING,)),
                 pltpu.SemaphoreType.DMA((8,)),

time: 111 us -> 111 us (level)
  no operation moved by 1% of the time
where the time goes in v11:
time: 111 us; the launch traced here: 110 us
  Pallas kernels  109 us (98%)
    pallas_call x1, Pallas kernels, local_forward(): pl.pallas_call(kernel, out_shape=[pltpu.VMEM((32, 16, 32, 64), f32)] * 2...  103 us
    pallas_call x1, Pallas kernels, local_forward(): pl.pallas_call(put, out_shape=[jax.ShapeDtypeStruct((32, 16, 32, 64), f32...  5.94 us

profile of v11, /device:TPU:1, one launch (start us, length us, event | category | flops | bytes accessed | tf_op | source)
XLA Modules:
  0.0 109.7 jit_solution(3204312096790472585)
XLA Ops:
  0.6 103.1 %dft3.1 = (f32[32,16,32,64]{3,2,1,0:T(8,128)S(1)}, f32[32,16,32,64]{3,2,1,0:T(8,128)S(1)}, f32[512,512]{1,0:T(8,128)S(1)}, f32[256,512]{1,0:T(8,128)S(1)}, f32[512,128]{1,0:T(8,128)S(1)}) custom-call(f32[8,4,16,32,64]{4,3,2,1,0:T(8,128)} %bitcast.6, f32[8,4,16,32,64]{4,3,2,1,0:T(8,128)} %bitcast.7, f32[16,32,64]{2,1,0:T(8,128)} %gf.1, ...), custom_call_target="tpu_custom_call" | custom-call | tf_op jit(solution)/shard_map/dft3/pallas_call | solution.py:303
  103.7 5.9 %put.1 = (f32[32,16,32,64]{3,2,1,0:T(8,128)}, f32[32,16,32,64]{3,2,1,0:T(8,128)}) custom-call(f32[32,16,32,64]{3,2,1,0:T(8,128)S(1)} %get-tuple-element.7.vr, f32[32,16,32,64]{3,2,1,0:T(8,128)S(1)} %get-tuple-element.8.vi, f32[512,512]{1,0:T(8,128)S(1)} %get-tuple-element.9.mat, f32[256,512]{1,0:T(8,128)S(1)} %get-tuple-element.10.last, ...), custom_call_target="tpu_custom_call" | custom-call | tf_op jit(solution)/shard_map/put/pallas_call | solution.py:332

commit v12 on v11

--- a/solution.py
+++ b/solution.py
@@ -11,7 +11,7 @@
 
 MESH = pl.DeviceIdType.MESH
 HALF = math.sqrt(0.5)
-GROUPS, PACK, UNITS, RING = 8, 4, 32, 4
+GROUPS, PACK, UNITS, RING, LAG = 8, 4, 32, 4, 7
 
 
 def interleave(even, odd):
@@ -239,9 +239,12 @@
     gain = gs[...].reshape(512, 64)
     gv[...] = jnp.concatenate([gain, gain], axis=1)
 
-    @pl.loop(1, UNITS)
+    @pl.loop(1, UNITS + LAG - 3)
     def _(t):
-        step_y(t)
+        @pl.when(t < UNITS)
+        def _():
+            step_y(t)
+
         g, i = (t + 7) // 4, lax.rem(t + 3, 4)
 
         @pl.when(g < GROUPS)
@@ -262,9 +265,9 @@
                     load(g + RING, 0).start()
                     load(g + RING, 1).start()
 
-        @pl.when((t >= 3) & (lax.rem(t, 2) == 1))
+        @pl.when((t >= LAG) & (lax.rem(t - LAG, 2) == 0))
         def _():
-            step_z((t - 3) // 2)
+            step_z((t - LAG) // 2)
 
     @pl.loop(0, UNITS)
     def _(u):

time: 111 us -> 111 us (level)
  no operation moved by 1% of the time
where the time goes in v12:
time: 111 us; the launch traced here: 110 us
  Pallas kernels  109 us (98%)
    pallas_call x1, Pallas kernels, local_forward(): pl.pallas_call(kernel, out_shape=[pltpu.VMEM((32, 16, 32, 64), f32)] * 2...  103 us
    pallas_call x1, Pallas kernels, local_forward(): pl.pallas_call(put, out_shape=[jax.ShapeDtypeStruct((32, 16, 32, 64), f32...  5.94 us

profile of v12, /device:TPU:1, one launch (start us, length us, event | category | flops | bytes accessed | tf_op | source)
XLA Modules:
  0.0 109.7 jit_solution(7009334152794628375)
XLA Ops:
  0.6 103.1 %dft3.1 = (f32[32,16,32,64]{3,2,1,0:T(8,128)S(1)}, f32[32,16,32,64]{3,2,1,0:T(8,128)S(1)}, f32[512,512]{1,0:T(8,128)S(1)}, f32[256,512]{1,0:T(8,128)S(1)}, f32[512,128]{1,0:T(8,128)S(1)}) custom-call(f32[8,4,16,32,64]{4,3,2,1,0:T(8,128)} %bitcast.6, f32[8,4,16,32,64]{4,3,2,1,0:T(8,128)} %bitcast.7, f32[16,32,64]{2,1,0:T(8,128)} %gf.1, ...), custom_call_target="tpu_custom_call" | custom-call | tf_op jit(solution)/shard_map/dft3/pallas_call | solution.py:306
  103.7 5.9 %put.1 = (f32[32,16,32,64]{3,2,1,0:T(8,128)}, f32[32,16,32,64]{3,2,1,0:T(8,128)}) custom-call(f32[32,16,32,64]{3,2,1,0:T(8,128)S(1)} %get-tuple-element.7.vr, f32[32,16,32,64]{3,2,1,0:T(8,128)S(1)} %get-tuple-element.8.vi, f32[512,512]{1,0:T(8,128)S(1)} %get-tuple-element.9.mat, f32[256,512]{1,0:T(8,128)S(1)} %get-tuple-element.10.last, ...), custom_call_target="tpu_custom_call" | custom-call | tf_op jit(solution)/shard_map/put/pallas_call | solution.py:335

commit v13 on v12

--- a/solution.py
+++ b/solution.py
@@ -208,8 +208,8 @@
         if i == 0:
             pl.semaphore_wait(barrier, 4)
         send_row(0, 1, first, count).start()
+        send_row(0, 2, first, count).start()
     send_row(0, 0).start()
-    send_row(0, 2).start()
 
     def send_rows(first, last):
         @pl.loop(first, last)
@@ -231,7 +231,6 @@
         load(RING, k).start()
         load(1, k).wait()
     step_x(1, 0, 16)
-    send_rows(4, 8)
     for k in range(2):
         load(RING + 1, k).start()
     for copy in consts[1:]:
@@ -245,6 +244,10 @@
         def _():
             step_y(t)
 
+        @pl.when(t < UNITS - 3)
+        def _():
+            send_rows(t + 3, t + 4)
+
         g, i = (t + 7) // 4, lax.rem(t + 3, 4)
 
         @pl.when(g < GROUPS)
@@ -258,8 +261,6 @@
 
             @pl.when(i == 3)
             def _():
-                send_rows(4 * g, 4 * g + 4)
-
                 @pl.when(g + RING < GROUPS)
                 def _():
                     load(g + RING, 0).start()

time: 111 us -> 111 us (level)
  no operation moved by 1% of the time
where the time goes in v13:
time: 111 us; the launch traced here: 110 us
  Pallas kernels  109 us (98%)
    pallas_call x1, Pallas kernels, local_forward(): pl.pallas_call(kernel, out_shape=[pltpu.VMEM((32, 16, 32, 64), f32)] * 2...  103 us
    pallas_call x1, Pallas kernels, local_forward(): pl.pallas_call(put, out_shape=[jax.ShapeDtypeStruct((32, 16, 32, 64), f32...  5.94 us

profile of v13, /device:TPU:1, one launch (start us, length us, event | category | flops | bytes accessed | tf_op | source)
XLA Modules:
  0.0 109.7 jit_solution(11439912904744885928)
XLA Ops:
  0.6 103.2 %dft3.1 = (f32[32,16,32,64]{3,2,1,0:T(8,128)S(1)}, f32[32,16,32,64]{3,2,1,0:T(8,128)S(1)}, f32[512,512]{1,0:T(8,128)S(1)}, f32[256,512]{1,0:T(8,128)S(1)}, f32[512,128]{1,0:T(8,128)S(1)}) custom-call(f32[8,4,16,32,64]{4,3,2,1,0:T(8,128)} %bitcast.6, f32[8,4,16,32,64]{4,3,2,1,0:T(8,128)} %bitcast.7, f32[16,32,64]{2,1,0:T(8,128)} %gf.1, ...), custom_call_target="tpu_custom_call" | custom-call | tf_op jit(solution)/shard_map/dft3/pallas_call | solution.py:307
  103.8 5.9 %put.1 = (f32[32,16,32,64]{3,2,1,0:T(8,128)}, f32[32,16,32,64]{3,2,1,0:T(8,128)}) custom-call(f32[32,16,32,64]{3,2,1,0:T(8,128)S(1)} %get-tuple-element.7.vr, f32[32,16,32,64]{3,2,1,0:T(8,128)S(1)} %get-tuple-element.8.vi, f32[512,512]{1,0:T(8,128)S(1)} %get-tuple-element.9.mat, f32[256,512]{1,0:T(8,128)S(1)} %get-tuple-element.10.last, ...), custom_call_target="tpu_custom_call" | custom-call | tf_op jit(solution)/shard_map/put/pallas_call | solution.py:336

commit v14 on v9

--- a/solution.py
+++ b/solution.py
@@ -68,34 +68,33 @@
             outi[at(2 * n + f)] = pair[:, 64:].reshape(8, 32, 64)
 
 
-def kernel(ur, ui, gf, wz, tw, outr, outi, wv, last, gv, inr, ini, xbuf, b2, r2, tv, gs, asc, bsc, lsc,
+def kernel(ur, ui, gf, wz, tw, outr, outi, wv, last, gv, inp, xbuf, b2, r2, tv, gs, asc, bsc, lsc,
            in_sem, q_sem, c_sem, s1, d1, s2, d2):
     row, col = lax.axis_index("row"), lax.axis_index("col")
     core = lax.rem(row, 2)
     dests = [1 + 2 * core, 2 - core, 3 - core]
     other = 1 - col
 
-    barrier = pltpu.get_barrier_semaphore()
-    for p in (1, 2, 3):
-        pl.semaphore_signal(barrier, inc=1, device_id={"row": lax.rem(row + p, 4)}, device_id_type=MESH)
-    pl.semaphore_signal(barrier, inc=1, device_id={"col": other}, device_id_type=MESH)
+    def arrived(ref, sem):
+        pltpu.make_async_remote_copy(src_ref=ref, dst_ref=ref, send_sem=sem, recv_sem=sem,
+                                     device_id={"row": row}, device_id_type=MESH).wait_recv()
 
     def load(g, k):
-        src, dst = ((ur, inr), (ui, ini))[k]
-        return pltpu.make_async_copy(src.at[g], dst.at[lax.rem(g, RING)], in_sem.at[2 * lax.rem(g, RING) + k])
+        src, dst = (ur, ui)[k], inp.at[k]
+        return pltpu.make_async_copy(src.at[g], dst.at[lax.rem(g, RING)], in_sem.at[lax.rem(g, RING)])
 
     pieces = ((0, 2), (2, 2), (4, 4), (8, 8))
 
     def piece(i, k):
-        src, dst = ((ur, inr), (ui, ini))[k]
+        src, dst = (ur, ui)[k], inp.at[k]
         part = (0, slice(None), pl.ds(*pieces[i]))
-        return pltpu.make_async_copy(src.at[part], dst.at[part], q_sem.at[2 * i + k])
+        return pltpu.make_async_copy(src.at[part], dst.at[part], q_sem.at[i])
 
     consts = [
         pltpu.make_async_copy(tw, tv, c_sem.at[0]),
         pltpu.make_async_copy(wz.at[col], wv.at[pl.ds(0, 256)], c_sem.at[1]),
-        pltpu.make_async_copy(wz.at[other], wv.at[pl.ds(256, 256)], c_sem.at[2]),
-        pltpu.make_async_copy(gf, gs, c_sem.at[3]),
+        pltpu.make_async_copy(wz.at[other], wv.at[pl.ds(256, 256)], c_sem.at[1]),
+        pltpu.make_async_copy(gf, gs, c_sem.at[2]),
     ]
     for i in range(4):
         piece(i, 0).start()
@@ -103,14 +102,19 @@
         if i == 0:
             consts[0].start()
 
+    barrier = pltpu.get_barrier_semaphore()
+    for p in (1, 2, 3):
+        pl.semaphore_signal(barrier, inc=1, device_id={"row": lax.rem(row + p, 4)}, device_id_type=MESH)
+    pl.semaphore_signal(barrier, inc=1, device_id={"col": other}, device_id_type=MESH)
+
     def step_x(g, first, count):
         ring = lax.rem(g, RING)
         slots = [3 + lax.rem(k + 4 - row, 4) for k in range(4)]
         bases = [[(2 * g + t) * 7 + slots[k] for t in range(2)] for k in range(4)]
 
         def one(y, s):
-            ar = inr[ring, :, y].reshape(PACK * 32, 64).T
-            ai = ini[ring, :, y].reshape(PACK * 32, 64).T
+            ar = inp[0, ring, :, y].reshape(PACK * 32, 64).T
+            ai = inp[1, ring, :, y].reshape(PACK * 32, 64).T
             a = dft8([(ar[8 * j : 8 * j + 8], ai[8 * j : 8 * j + 8]) for j in range(8)])
             for k1 in range(8):
                 vr, vi = times(a[k1], tv[0, k1], tv[1, k1])
@@ -130,19 +134,13 @@
         p = dests[j]
         return pltpu.make_async_remote_copy(
             src_ref=xbuf.at[u * 7 + 3 + p, pl.ds(first, count)], dst_ref=xbuf.at[u * 7 + 3 - p, pl.ds(first, count)],
-            send_sem=s1.at[u * 3 + j], recv_sem=d1.at[u * 3 + 3 - p],
+            send_sem=s1, recv_sem=d1.at[u],
             device_id={"row": lax.rem(row + p, 4)}, device_id_type=MESH)
-
-    def wait_row(u, slot):
-        part = xbuf.at[u * 7 + slot]
-        pltpu.make_async_remote_copy(
-            src_ref=part, dst_ref=part, send_sem=s1.at[u * 3], recv_sem=d1.at[u * 3 + slot],
-            device_id={"row": row}, device_id_type=MESH).wait_recv()
 
     def send_col(u):
         return pltpu.make_async_remote_copy(
             src_ref=b2.at[pl.ds(u * 4 + 2 * other, 2)], dst_ref=r2.at[pl.ds(u * 2, 2)],
-            send_sem=s2.at[u], recv_sem=d2.at[u], device_id={"col": other}, device_id_type=MESH)
+            send_sem=s2, recv_sem=d2.at[u], device_id={"col": other}, device_id_type=MESH)
 
     def step_y(u):
         slots = [u * 7 + lax.rem(r + 7 - row, 4) for r in range(4)]
@@ -171,8 +169,7 @@
 
     consts[0].wait()
     for i, (first, count) in enumerate(pieces):
-        piece(i, 0).wait()
-        piece(i, 1).wait()
+        arrived(inp.at[:, 0, :, pl.ds(first, count)], q_sem.at[i])
         step_x(0, first, count)
         if i == 0:
             pl.semaphore_wait(barrier, 4)
@@ -193,8 +190,7 @@
     def _(t):
         @pl.when(t < UNITS)
         def _():
-            for slot in range(3):
-                wait_row(t, slot)
+            arrived(xbuf.at[pl.ds(t * 7, 3)], d1.at[t])
             step_y(t)
             send_col(t).start()
 
@@ -202,15 +198,15 @@
         def _():
             for k in range(2):
                 load(RING, k).start()
-                load(1, k).wait()
+            arrived(inp.at[:, 1], in_sem.at[1])
             step_x(1, 0, 16)
             for u in (2, 3):
                 for j in range(3):
                     send_row(u, j).start()
             for k in range(2):
                 load(RING + 1, k).start()
-            for copy in consts[1:]:
-                copy.wait()
+            arrived(wv, c_sem.at[1])
+            consts[3].wait()
             gain = gs[...].reshape(512, 64)
             gv[...] = jnp.concatenate([gain, gain], axis=1)
 
@@ -222,8 +218,7 @@
 
             @pl.when(half == 0)
             def _():
-                load(g, 0).wait()
-                load(g, 1).wait()
+                arrived(inp.at[:, lax.rem(g, RING)], in_sem.at[lax.rem(g, RING)])
 
             step_x(g, 8 * half, 8)
 
@@ -244,29 +239,20 @@
             send_col(u).wait_recv()
             step_z(u)
 
-    @pl.loop(0, UNITS)
-    def _(u):
-        for j in range(3):
-            send_row(u, j).wait_send()
-
-    @pl.loop(0, UNITS - 1)
-    def _(u):
-        send_col(u).wait_send()
-
+    arrived(xbuf.at[pl.ds(0, 3 * UNITS)], s1)
     send_col(UNITS - 1).wait_recv()
     gather_z(UNITS - 1, last)
-    send_col(UNITS - 1).wait_send()
+    arrived(b2.at[pl.ds(0, 2 * UNITS)], s2)
 
 
 def put(vr, vi, mat, last, gain, outr, outi, lr, li, sem):
     cuts = [(pl.ds(7 * i, 7), slice(None)) for i in range(4)] + [(pl.ds(28, 4), pl.ds(0, 8))]
-    copies = [pltpu.make_async_copy(v.at[cut], o.at[cut], sem.at[2 * i + k])
-              for i, cut in enumerate(cuts) for k, (v, o) in enumerate(((vr, outr), (vi, outi)))]
+    copies = [pltpu.make_async_copy(v.at[cut], o.at[cut], sem) for cut in cuts for v, o in ((vr, outr), (vi, outi))]
     for copy in copies:
         copy.start()
     lane_product(last, mat, gain[256:, :], lr, li, lambda f: f)
     cut = (pl.ds(28, 4), pl.ds(8, 8))
-    tail = [pltpu.make_async_copy(v, o.at[cut], sem.at[10 + k]) for k, (v, o) in enumerate(((lr, outr), (li, outi)))]
+    tail = [pltpu.make_async_copy(v, o.at[cut], sem) for v, o in ((lr, outr), (li, outi))]
     for copy in tail:
         copy.start()
     for copy in copies + tail:
@@ -285,8 +271,7 @@
             in_specs=[pl.BlockSpec(memory_space=pltpu.HBM)] * 5,
             out_specs=[pl.BlockSpec(memory_space=pltpu.VMEM)] * 5,
             scratch_shapes=[
-                pltpu.VMEM((RING, PACK, 16, 32, 64), f32),
-                pltpu.VMEM((RING, PACK, 16, 32, 64), f32),
+                pltpu.VMEM((2, RING, PACK, 16, 32, 64), f32),
                 pltpu.VMEM((UNITS * 7, 16, 2, 8, 128), f32),
                 pltpu.VMEM((UNITS * 4, 256, 128), f32),
                 pltpu.VMEM((UNITS * 2, 256, 128), f32),
@@ -295,12 +280,12 @@
                 pltpu.VMEM((2, 2, 64, 128), f32),
                 pltpu.VMEM((8, 8, 2, 8, 128), f32),
                 pltpu.VMEM((256, 512), f32),
-                pltpu.SemaphoreType.DMA((2 * RING,)),
-                pltpu.SemaphoreType.DMA((8,)),
+                pltpu.SemaphoreType.DMA((RING,)),
                 pltpu.SemaphoreType.DMA((4,)),
-                pltpu.SemaphoreType.DMA((3 * UNITS,)),
-                pltpu.SemaphoreType.DMA((3 * UNITS,)),
+                pltpu.SemaphoreType.DMA((3,)),
+                pltpu.SemaphoreType.DMA,
                 pltpu.SemaphoreType.DMA((UNITS,)),
+                pltpu.SemaphoreType.DMA,
                 pltpu.SemaphoreType.DMA((UNITS,)),
             ],
             compiler_params=pltpu.CompilerParams(
@@ -312,7 +297,7 @@
             out_shape=[jax.ShapeDtypeStruct((32, 16, 32, 64), f32)] * 2,
             in_specs=[pl.BlockSpec(memory_space=pltpu.VMEM)] * 5,
             out_specs=[pl.BlockSpec(memory_space=pltpu.HBM)] * 2,
-            scratch_shapes=[pltpu.VMEM((PACK, 8, 32, 64), f32)] * 2 + [pltpu.SemaphoreType.DMA((12,))],
+            scratch_shapes=[pltpu.VMEM((PACK, 8, 32, 64), f32)] * 2 + [pltpu.SemaphoreType.DMA],
             compiler_params=pltpu.CompilerParams(vmem_limit_bytes=8 * 1024 * 1024),
             name="put",
         )(*spectrum)

time: 109 us -> 108 us (level)
  Pallas kernels: 109 us -> 107 us
where the time goes in v14:
time: 108 us
  Pallas kernels  107 us (99%)
    pallas_call x1, Pallas kernels, local_forward(): pl.pallas_call(kernel, out_shape=[pltpu.VMEM((32, 16, 32, 64), f32)] * 2...  102 us
    pallas_call x1, Pallas kernels, local_forward(): pl.pallas_call(put, out_shape=[jax.ShapeDtypeStruct((32, 16, 32, 64), f32...  5.84 us

profile of v14, /device:TPU:1, one launch (start us, length us, event | category | flops | bytes accessed | tf_op | source)
XLA Modules:
  0.0 108.1 jit_solution(8035882511646621267)
XLA Ops:
  0.6 101.6 %dft3.1 = (f32[32,16,32,64]{3,2,1,0:T(8,128)S(1)}, f32[32,16,32,64]{3,2,1,0:T(8,128)S(1)}, f32[512,512]{1,0:T(8,128)S(1)}, f32[256,512]{1,0:T(8,128)S(1)}, f32[512,128]{1,0:T(8,128)S(1)}) custom-call(f32[8,4,16,32,64]{4,3,2,1,0:T(8,128)} %bitcast.6, f32[8,4,16,32,64]{4,3,2,1,0:T(8,128)} %bitcast.7, f32[16,32,64]{2,1,0:T(8,128)} %gf.1, ...), custom_call_target="tpu_custom_call" | custom-call | tf_op jit(solution)/shard_map/dft3/pallas_call | solution.py:267
  102.3 5.8 %put.1 = (f32[32,16,32,64]{3,2,1,0:T(8,128)}, f32[32,16,32,64]{3,2,1,0:T(8,128)}) custom-call(f32[32,16,32,64]{3,2,1,0:T(8,128)S(1)} %get-tuple-element.7.vr, f32[32,16,32,64]{3,2,1,0:T(8,128)S(1)} %get-tuple-element.8.vi, f32[512,512]{1,0:T(8,128)S(1)} %get-tuple-element.9.mat, f32[256,512]{1,0:T(8,128)S(1)} %get-tuple-element.10.last, ...), custom_call_target="tpu_custom_call" | custom-call | tf_op jit(solution)/shard_map/put/pallas_call | solution.py:295

commit v15 on v12

--- a/solution.py
+++ b/solution.py
@@ -92,34 +92,33 @@
             outi[at(2 * n + f)] = pair[:, 64:].reshape(8, 32, 64)
 
 
-def kernel(ur, ui, gf, wz, tw, outr, outi, wv, last, gv, inr, ini, xbuf, b2, r2, tv, gs, asc, bsc, lsc,
+def kernel(ur, ui, gf, wz, tw, outr, outi, wv, last, gv, inp, xbuf, b2, r2, tv, gs, asc, bsc, lsc,
            in_sem, q_sem, c_sem, s1, d1, s2, d2):
     row, col = lax.axis_index("row"), lax.axis_index("col")
     core = lax.rem(row, 2)
     dests = [1 + 2 * core, 2 - core, 3 - core]
     other = 1 - col
 
-    barrier = pltpu.get_barrier_semaphore()
-    for p in (1, 2, 3):
-        pl.semaphore_signal(barrier, inc=1, device_id={"row": lax.rem(row + p, 4)}, device_id_type=MESH)
-    pl.semaphore_signal(barrier, inc=1, device_id={"col": other}, device_id_type=MESH)
+    def arrived(ref, sem):
+        pltpu.make_async_remote_copy(src_ref=ref, dst_ref=ref, send_sem=sem, recv_sem=sem,
+                                     device_id={"row": row}, device_id_type=MESH).wait_recv()
 
     def load(g, k):
-        src, dst = ((ur, inr), (ui, ini))[k]
-        return pltpu.make_async_copy(src.at[g], dst.at[lax.rem(g, RING)], in_sem.at[2 * lax.rem(g, RING) + k])
+        src, dst = (ur, ui)[k], inp.at[k]
+        return pltpu.make_async_copy(src.at[g], dst.at[lax.rem(g, RING)], in_sem.at[lax.rem(g, RING)])
 
     pieces = ((0, 2), (2, 2), (4, 4), (8, 8))
 
     def piece(i, k):
-        src, dst = ((ur, inr), (ui, ini))[k]
+        src, dst = (ur, ui)[k], inp.at[k]
         part = (0, slice(None), pl.ds(*pieces[i]))
-        return pltpu.make_async_copy(src.at[part], dst.at[part], q_sem.at[2 * i + k])
+        return pltpu.make_async_copy(src.at[part], dst.at[part], q_sem.at[i])
 
     consts = [
         pltpu.make_async_copy(tw, tv, c_sem.at[0]),
         pltpu.make_async_copy(wz.at[col], wv.at[pl.ds(0, 256)], c_sem.at[1]),
-        pltpu.make_async_copy(wz.at[other], wv.at[pl.ds(256, 256)], c_sem.at[2]),
-        pltpu.make_async_copy(gf, gs, c_sem.at[3]),
+        pltpu.make_async_copy(wz.at[other], wv.at[pl.ds(256, 256)], c_sem.at[1]),
+        pltpu.make_async_copy(gf, gs, c_sem.at[2]),
     ]
     for i in range(4):
         piece(i, 0).start()
@@ -127,14 +126,19 @@
         if i == 0:
             consts[0].start()
 
+    barrier = pltpu.get_barrier_semaphore()
+    for p in (1, 2, 3):
+        pl.semaphore_signal(barrier, inc=1, device_id={"row": lax.rem(row + p, 4)}, device_id_type=MESH)
+    pl.semaphore_signal(barrier, inc=1, device_id={"col": other}, device_id_type=MESH)
+
     def step_x(g, first, count):
         ring = lax.rem(g, RING)
         bases = [4 * g * 7 + 3 + lax.rem(k + 4 - row, 4) for k in range(4)]
 
         def one(i, s):
             y = first + 2 * i + s
-            ar = inr[ring, :, y].reshape(PACK * 32, 64).T
-            ai = ini[ring, :, y].reshape(PACK * 32, 64).T
+            ar = inp[0, ring, :, y].reshape(PACK * 32, 64).T
+            ai = inp[1, ring, :, y].reshape(PACK * 32, 64).T
             a = dft8([(ar[8 * j : 8 * j + 8], ai[8 * j : 8 * j + 8]) for j in range(8)])
             for k1 in range(8):
                 vr, vi = times(a[k1], tv[0, k1], tv[1, k1])
@@ -156,23 +160,16 @@
         p = dests[j]
         return pltpu.make_async_remote_copy(
             src_ref=xbuf.at[u * 7 + 3 + p, pl.ds(first, count)], dst_ref=xbuf.at[u * 7 + 3 - p, pl.ds(first, count)],
-            send_sem=s1.at[u * 3 + j], recv_sem=d1.at[u * 3 + 3 - p],
+            send_sem=s1, recv_sem=d1.at[u],
             device_id={"row": lax.rem(row + p, 4)}, device_id_type=MESH)
-
-    def wait_row(u, slot):
-        part = xbuf.at[u * 7 + slot]
-        pltpu.make_async_remote_copy(
-            src_ref=part, dst_ref=part, send_sem=s1.at[u * 3], recv_sem=d1.at[u * 3 + slot],
-            device_id={"row": row}, device_id_type=MESH).wait_recv()
 
     def send_col(u):
         return pltpu.make_async_remote_copy(
             src_ref=b2.at[u * 2 + other], dst_ref=r2.at[u],
-            send_sem=s2.at[u], recv_sem=d2.at[u], device_id={"col": other}, device_id_type=MESH)
+            send_sem=s2, recv_sem=d2.at[u], device_id={"col": other}, device_id_type=MESH)
 
     def step_y(u):
-        for slot in range(3):
-            wait_row(u, slot)
+        arrived(xbuf.at[pl.ds(u * 7, 3)], d1.at[u])
         slots = [u * 7 + lax.rem(r + 7 - row, 4) for r in range(4)]
         for y2 in range(8):
             a = packed_dft8([xbuf[slots[y1 // 2], 8 * (y1 % 2) + y2] for y1 in range(8)])
@@ -202,8 +199,7 @@
 
     consts[0].wait()
     for i, (first, count) in enumerate(pieces):
-        piece(i, 0).wait()
-        piece(i, 1).wait()
+        arrived(inp.at[:, 0, :, pl.ds(first, count)], q_sem.at[i])
         step_x(0, first, count)
         if i == 0:
             pl.semaphore_wait(barrier, 4)
@@ -229,13 +225,13 @@
     step_y(0)
     for k in range(2):
         load(RING, k).start()
-        load(1, k).wait()
+    arrived(inp.at[:, 1], in_sem.at[1])
     step_x(1, 0, 16)
     send_rows(4, 8)
     for k in range(2):
         load(RING + 1, k).start()
-    for copy in consts[1:]:
-        copy.wait()
+    arrived(wv, c_sem.at[1])
+    consts[3].wait()
     gain = gs[...].reshape(512, 64)
     gv[...] = jnp.concatenate([gain, gain], axis=1)
 
@@ -251,8 +247,7 @@
         def _():
             @pl.when(i == 0)
             def _():
-                load(g, 0).wait()
-                load(g, 1).wait()
+                arrived(inp.at[:, lax.rem(g, RING)], in_sem.at[lax.rem(g, RING)])
 
             step_x(g, 4 * i, 4)
 
@@ -269,29 +264,19 @@
         def _():
             step_z((t - LAG) // 2)
 
-    @pl.loop(0, UNITS)
-    def _(u):
-        for j in range(3):
-            send_row(u, j).wait_send()
-
-    @pl.loop(0, UNITS - 2)
-    def _(u):
-        send_col(u).wait_send()
-
+    arrived(xbuf.at[pl.ds(0, 3 * UNITS)], s1)
     gather_z(UNITS - 2, last)
-    send_col(UNITS - 2).wait_send()
-    send_col(UNITS - 1).wait_send()
+    arrived(b2.at[pl.ds(0, UNITS)], s2)
 
 
 def put(vr, vi, mat, last, gain, outr, outi, lr, li, sem):
     cuts = [(pl.ds(7 * i, 7), slice(None)) for i in range(4)] + [(pl.ds(28, 4), pl.ds(0, 8))]
-    copies = [pltpu.make_async_copy(v.at[cut], o.at[cut], sem.at[2 * i + k])
-              for i, cut in enumerate(cuts) for k, (v, o) in enumerate(((vr, outr), (vi, outi)))]
+    copies = [pltpu.make_async_copy(v.at[cut], o.at[cut], sem) for cut in cuts for v, o in ((vr, outr), (vi, outi))]
     for copy in copies:
         copy.start()
     lane_product(last, mat, gain[256:, :], lr, li, lambda f: f)
     cut = (pl.ds(28, 4), pl.ds(8, 8))
-    tail = [pltpu.make_async_copy(v, o.at[cut], sem.at[10 + k]) for k, (v, o) in enumerate(((lr, outr), (li, outi)))]
+    tail = [pltpu.make_async_copy(v, o.at[cut], sem) for v, o in ((lr, outr), (li, outi))]
     for copy in tail:
         copy.start()
     for copy in copies + tail:
@@ -310,8 +295,7 @@
             in_specs=[pl.BlockSpec(memory_space=pltpu.HBM)] * 5,
             out_specs=[pl.BlockSpec(memory_space=pltpu.VMEM)] * 5,
             scratch_shapes=[
-                pltpu.VMEM((RING, PACK, 16, 32, 64), f32),
-                pltpu.VMEM((RING, PACK, 16, 32, 64), f32),
+                pltpu.VMEM((2, RING, PACK, 16, 32, 64), f32),
                 pltpu.VMEM((UNITS * 7, 16, 8, 128), f32),
                 pltpu.VMEM((UNITS * 2, 256, 128), f32),
                 pltpu.VMEM((UNITS, 256, 128), f32),
@@ -320,12 +304,12 @@
                 pltpu.VMEM((2, 2, 64, 128), f32),
                 pltpu.VMEM((8, 8, 8, 128), f32),
                 pltpu.VMEM((256, 512), f32),
-                pltpu.SemaphoreType.DMA((2 * RING,)),
-                pltpu.SemaphoreType.DMA((8,)),
+                pltpu.SemaphoreType.DMA((RING,)),
                 pltpu.SemaphoreType.DMA((4,)),
-                pltpu.SemaphoreType.DMA((3 * UNITS,)),
-                pltpu.SemaphoreType.DMA((3 * UNITS,)),
+                pltpu.SemaphoreType.DMA((3,)),
+                pltpu.SemaphoreType.DMA,
                 pltpu.SemaphoreType.DMA((UNITS,)),
+                pltpu.SemaphoreType.DMA,
                 pltpu.SemaphoreType.DMA((UNITS,)),
             ],
             compiler_params=pltpu.CompilerParams(
@@ -337,7 +321,7 @@
             out_shape=[jax.ShapeDtypeStruct((32, 16, 32, 64), f32)] * 2,
             in_specs=[pl.BlockSpec(memory_space=pltpu.VMEM)] * 5,
             out_specs=[pl.BlockSpec(memory_space=pltpu.HBM)] * 2,
-            scratch_shapes=[pltpu.VMEM((PACK, 8, 32, 64), f32)] * 2 + [pltpu.SemaphoreType.DMA((12,))],
+            scratch_shapes=[pltpu.VMEM((PACK, 8, 32, 64), f32)] * 2 + [pltpu.SemaphoreType.DMA],
             compiler_params=pltpu.CompilerParams(vmem_limit_bytes=8 * 1024 * 1024),
             name="put",
         )(*spectrum)

time: 111 us -> 109 us (0.982)
  Pallas kernels: 109 us -> 107 us
    pallas_call x1, Pallas kernels: 103 us -> 101 us  [local_forward(): pl.pallas_call(kernel, out_shape=[pltpu.VMEM((32, 16, 32, 64), f32)] * 2...]
where the time goes in v15:
time: 109 us; the launch traced here: 108 us
  Pallas kernels  107 us (98%)
    pallas_call x1, Pallas kernels, local_forward(): pl.pallas_call(kernel, out_shape=[pltpu.VMEM((32, 16, 32, 64), f32)] * 2...  101 us
    pallas_call x1, Pallas kernels, local_forward(): pl.pallas_call(put, out_shape=[jax.ShapeDtypeStruct((32, 16, 32, 64), f32...  5.84 us

profile of v15, /device:TPU:1, one launch (start us, length us, event | category | flops | bytes accessed | tf_op | source)
XLA Modules:
  0.0 107.7 jit_solution(1710002185374370130)
XLA Ops:
  0.6 101.3 %dft3.1 = (f32[32,16,32,64]{3,2,1,0:T(8,128)S(1)}, f32[32,16,32,64]{3,2,1,0:T(8,128)S(1)}, f32[512,512]{1,0:T(8,128)S(1)}, f32[256,512]{1,0:T(8,128)S(1)}, f32[512,128]{1,0:T(8,128)S(1)}) custom-call(f32[8,4,16,32,64]{4,3,2,1,0:T(8,128)} %bitcast.6, f32[8,4,16,32,64]{4,3,2,1,0:T(8,128)} %bitcast.7, f32[16,32,64]{2,1,0:T(8,128)} %gf.1, ...), custom_call_target="tpu_custom_call" | custom-call | tf_op jit(solution)/shard_map/dft3/pallas_call | solution.py:291
  101.9 5.8 %put.1 = (f32[32,16,32,64]{3,2,1,0:T(8,128)}, f32[32,16,32,64]{3,2,1,0:T(8,128)}) custom-call(f32[32,16,32,64]{3,2,1,0:T(8,128)S(1)} %get-tuple-element.7.vr, f32[32,16,32,64]{3,2,1,0:T(8,128)S(1)} %get-tuple-element.8.vi, f32[512,512]{1,0:T(8,128)S(1)} %get-tuple-element.9.mat, f32[256,512]{1,0:T(8,128)S(1)} %get-tuple-element.10.last, ...), custom_call_target="tpu_custom_call" | custom-call | tf_op jit(solution)/shard_map/put/pallas_call | solution.py:319

commit v16 on v15

--- a/solution.py
+++ b/solution.py
@@ -11,7 +11,7 @@
 
 MESH = pl.DeviceIdType.MESH
 HALF = math.sqrt(0.5)
-GROUPS, PACK, UNITS, RING, LAG = 8, 4, 32, 4, 7
+GROUPS, PACK, UNITS, RING, LAG = 8, 4, 32, 4, 5
 
 
 def interleave(even, odd):
@@ -166,7 +166,7 @@
     def send_col(u):
         return pltpu.make_async_remote_copy(
             src_ref=b2.at[u * 2 + other], dst_ref=r2.at[u],
-            send_sem=s2, recv_sem=d2.at[u], device_id={"col": other}, device_id_type=MESH)
+            send_sem=s2, recv_sem=d2.at[u // 2], device_id={"col": other}, device_id_type=MESH)
 
     def step_y(u):
         arrived(xbuf.at[pl.ds(u * 7, 3)], d1.at[u])
@@ -182,18 +182,18 @@
                 b2[u * 2 + k2 // 4, pl.ds(8 * (k1 + 8 * (k2 % 4)), 8), :] = b[k2]
         send_col(u).start()
 
-    def gather_z(u, dst):
-        send_col(u).wait_recv()
-        send_col(u + 1).wait_recv()
-        for kx in range(8):
-            v = u + kx // 4
-            for q in range(2):
-                rows = pl.ds(4 * q + kx % 4, 32, stride=8)
-                dst[pl.ds(32 * kx, 32), pl.ds(128 * q, 128)] = b2[v * 2 + col, rows, :]
-                dst[pl.ds(32 * kx, 32), pl.ds(256 + 128 * q, 128)] = r2[v, rows, :]
+    def gather_z(m, dst):
+        def part(lane, plane):
+            for kx in range(8):
+                for q in range(2):
+                    dst[pl.ds(32 * kx, 32), pl.ds(lane + 128 * q, 128)] = plane(2 * m + kx // 4, pl.ds(4 * q + kx % 4, 32, stride=8))
+
+        part(0, lambda u, rows: b2[u * 2 + col, rows, :])
+        arrived(r2.at[pl.ds(2 * m, 2)], d2.at[m])
+        part(256, lambda u, rows: r2[u, rows, :])
 
     def step_z(m):
-        gather_z(2 * m, lsc)
+        gather_z(m, lsc)
         gain = gv[pl.ds(pl.multiple_of(256 * lax.rem(m, 2), 256), 256), :]
         lane_product(lsc, wv, gain, outr, outi, lambda f: (PACK * (m // 2) + f, pl.ds(8 * lax.rem(m, 2), 8)))
 
@@ -204,16 +204,21 @@
         if i == 0:
             pl.semaphore_wait(barrier, 4)
         send_row(0, 1, first, count).start()
+        if i == 1:
+            send_row(1, 1, 0, first + count).start()
     send_row(0, 0).start()
+    send_row(1, 1, 4, 12).start()
+    send_row(1, 0).start()
     send_row(0, 2).start()
 
     def send_rows(first, last):
         @pl.loop(first, last)
         def _(u):
-            for j in range(3):
-                send_row(u, j).start()
-
-    send_rows(1, 4)
+            send_row(u, 1).start()
+            send_row(u, 0).start()
+            send_row(u - 1, 2).start()
+
+    send_rows(2, 4)
 
     @pl.loop(1, RING)
     def _(g):
@@ -255,6 +260,10 @@
             def _():
                 send_rows(4 * g, 4 * g + 4)
 
+                @pl.when(g == GROUPS - 1)
+                def _():
+                    send_row(UNITS - 1, 2).start()
+
                 @pl.when(g + RING < GROUPS)
                 def _():
                     load(g + RING, 0).start()
@@ -265,7 +274,7 @@
             step_z((t - LAG) // 2)
 
     arrived(xbuf.at[pl.ds(0, 3 * UNITS)], s1)
-    gather_z(UNITS - 2, last)
+    gather_z(UNITS // 2 - 1, last)
     arrived(b2.at[pl.ds(0, UNITS)], s2)
 
 
@@ -310,7 +319,7 @@
                 pltpu.SemaphoreType.DMA,
                 pltpu.SemaphoreType.DMA((UNITS,)),
                 pltpu.SemaphoreType.DMA,
-                pltpu.SemaphoreType.DMA((UNITS,)),
+                pltpu.SemaphoreType.DMA((UNITS // 2,)),
             ],
             compiler_params=pltpu.CompilerParams(
                 collective_id=0, has_side_effects=True, vmem_limit_bytes=40 * 1024 * 1024),

time: 109 us -> 108 us (level)
  no operation moved by 1% of the time
where the time goes in v16:
time: 108 us
  Pallas kernels  107 us (99%)
    pallas_call x1, Pallas kernels, local_forward(): pl.pallas_call(kernel, out_shape=[pltpu.VMEM((32, 16, 32, 64), f32)] * 2...  101 us
    pallas_call x1, Pallas kernels, local_forward(): pl.pallas_call(put, out_shape=[jax.ShapeDtypeStruct((32, 16, 32, 64), f32...  5.84 us

profile of v16, /device:TPU:1, one launch (start us, length us, event | category | flops | bytes accessed | tf_op | source)
XLA Modules:
  0.0 107.6 jit_solution(6761276296044533969)
XLA Ops:
  0.6 101.2 %dft3.1 = (f32[32,16,32,64]{3,2,1,0:T(8,128)S(1)}, f32[32,16,32,64]{3,2,1,0:T(8,128)S(1)}, f32[512,512]{1,0:T(8,128)S(1)}, f32[256,512]{1,0:T(8,128)S(1)}, f32[512,128]{1,0:T(8,128)S(1)}) custom-call(f32[8,4,16,32,64]{4,3,2,1,0:T(8,128)} %bitcast.6, f32[8,4,16,32,64]{4,3,2,1,0:T(8,128)} %bitcast.7, f32[16,32,64]{2,1,0:T(8,128)} %gf.1, ...), custom_call_target="tpu_custom_call" | custom-call | tf_op jit(solution)/shard_map/dft3/pallas_call | solution.py:300
  101.8 5.8 %put.1 = (f32[32,16,32,64]{3,2,1,0:T(8,128)}, f32[32,16,32,64]{3,2,1,0:T(8,128)}) custom-call(f32[32,16,32,64]{3,2,1,0:T(8,128)S(1)} %get-tuple-element.7.vr, f32[32,16,32,64]{3,2,1,0:T(8,128)S(1)} %get-tuple-element.8.vi, f32[512,512]{1,0:T(8,128)S(1)} %get-tuple-element.9.mat, f32[256,512]{1,0:T(8,128)S(1)} %get-tuple-element.10.last, ...), custom_call_target="tpu_custom_call" | custom-call | tf_op jit(solution)/shard_map/put/pallas_call | solution.py:328

commit v17 on v16

--- a/solution.py
+++ b/solution.py
@@ -92,7 +92,7 @@
             outi[at(2 * n + f)] = pair[:, 64:].reshape(8, 32, 64)
 
 
-def kernel(ur, ui, gf, wz, tw, outr, outi, wv, last, gv, inp, xbuf, b2, r2, tv, gs, asc, bsc, lsc,
+def body(ur, ui, gf, wz, tw, outr, outi, wv, last, gv, inp, xbuf, b2, r2, tv, gs, asc, bsc, lsc,
            in_sem, q_sem, c_sem, s1, d1, s2, d2):
     row, col = lax.axis_index("row"), lax.axis_index("col")
     core = lax.rem(row, 2)
@@ -276,6 +276,12 @@
     arrived(xbuf.at[pl.ds(0, 3 * UNITS)], s1)
     gather_z(UNITS // 2 - 1, last)
     arrived(b2.at[pl.ds(0, UNITS)], s2)
+
+
+def kernel(*refs):
+    dma = pltpu.SemaphoreType.DMA
+    pl.run_scoped(functools.partial(body, *refs), in_sem=dma((RING,)), q_sem=dma((4,)), c_sem=dma((3,)), s1=dma,
+                  d1=dma((UNITS,)), s2=dma, d2=dma((UNITS // 2,)))
 
 
 def put(vr, vi, mat, last, gain, outr, outi, lr, li, sem):
@@ -313,13 +319,6 @@
                 pltpu.VMEM((2, 2, 64, 128), f32),
                 pltpu.VMEM((8, 8, 8, 128), f32),
                 pltpu.VMEM((256, 512), f32),
-                pltpu.SemaphoreType.DMA((RING,)),
-                pltpu.SemaphoreType.DMA((4,)),
-                pltpu.SemaphoreType.DMA((3,)),
-                pltpu.SemaphoreType.DMA,
-                pltpu.SemaphoreType.DMA((UNITS,)),
-                pltpu.SemaphoreType.DMA,
-                pltpu.SemaphoreType.DMA((UNITS // 2,)),
             ],
             compiler_params=pltpu.CompilerParams(
                 collective_id=0, has_side_effects=True, vmem_limit_bytes=40 * 1024 * 1024),

time: 108 us -> 107 us (level)
  no operation moved by 1% of the time
where the time goes in v17:
time: 107 us
  Pallas kernels  106 us (99%)
    pallas_call x1, Pallas kernels, local_forward(): pl.pallas_call(kernel, out_shape=[pltpu.VMEM((32, 16, 32, 64), f32)] * 2...  101 us
    pallas_call x1, Pallas kernels, local_forward(): pl.pallas_call(put, out_shape=[jax.ShapeDtypeStruct((32, 16, 32, 64), f32...  5.84 us

profile of v17, /device:TPU:1, one launch (start us, length us, event | category | flops | bytes accessed | tf_op | source)
XLA Modules:
  0.0 107.1 jit_solution(10884564480101882739)
XLA Ops:
  0.6 100.6 %dft3.1 = (f32[32,16,32,64]{3,2,1,0:T(8,128)S(1)}, f32[32,16,32,64]{3,2,1,0:T(8,128)S(1)}, f32[512,512]{1,0:T(8,128)S(1)}, f32[256,512]{1,0:T(8,128)S(1)}, f32[512,128]{1,0:T(8,128)S(1)}) custom-call(f32[8,4,16,32,64]{4,3,2,1,0:T(8,128)} %bitcast.6, f32[8,4,16,32,64]{4,3,2,1,0:T(8,128)} %bitcast.7, f32[16,32,64]{2,1,0:T(8,128)} %refs_2_.1, ...), custom_call_target="tpu_custom_call" | custom-call | tf_op jit(solution)/shard_map/dft3/pallas_call | solution.py:306
  101.2 5.8 %put.1 = (f32[32,16,32,64]{3,2,1,0:T(8,128)}, f32[32,16,32,64]{3,2,1,0:T(8,128)}) custom-call(f32[32,16,32,64]{3,2,1,0:T(8,128)S(1)} %get-tuple-element.7.vr, f32[32,16,32,64]{3,2,1,0:T(8,128)S(1)} %get-tuple-element.8.vi, f32[512,512]{1,0:T(8,128)S(1)} %get-tuple-element.9.mat, f32[256,512]{1,0:T(8,128)S(1)} %get-tuple-element.10.last, ...), custom_call_target="tpu_custom_call" | custom-call | tf_op jit(solution)/shard_map/put/pallas_call | solution.py:327

commit v18 on v17

--- a/solution.py
+++ b/solution.py
@@ -120,16 +120,18 @@
         pltpu.make_async_copy(wz.at[other], wv.at[pl.ds(256, 256)], c_sem.at[1]),
         pltpu.make_async_copy(gf, gs, c_sem.at[2]),
     ]
-    for i in range(4):
+    def start_piece(i):
         piece(i, 0).start()
         piece(i, 1).start()
-        if i == 0:
-            consts[0].start()
-
+
+    consts[0].start()
+    start_piece(0)
     barrier = pltpu.get_barrier_semaphore()
     for p in (1, 2, 3):
         pl.semaphore_signal(barrier, inc=1, device_id={"row": lax.rem(row + p, 4)}, device_id_type=MESH)
     pl.semaphore_signal(barrier, inc=1, device_id={"col": other}, device_id_type=MESH)
+    for i in range(1, 4):
+        start_piece(i)
 
     def step_x(g, first, count):
         ring = lax.rem(g, RING)

time: 107 us -> 107 us (level)
  no operation moved by 1% of the time
where the time goes in v18:
time: 107 us
  Pallas kernels  106 us (99%)
    pallas_call x1, Pallas kernels, local_forward(): pl.pallas_call(kernel, out_shape=[pltpu.VMEM((32, 16, 32, 64), f32)] * 2...  100 us
    pallas_call x1, Pallas kernels, local_forward(): pl.pallas_call(put, out_shape=[jax.ShapeDtypeStruct((32, 16, 32, 64), f32...  5.84 us

profile of v18, /device:TPU:1, one launch (start us, length us, event | category | flops | bytes accessed | tf_op | source)
XLA Modules:
  0.0 106.7 jit_solution(12022900335713535254)
XLA Ops:
  0.6 100.2 %dft3.1 = (f32[32,16,32,64]{3,2,1,0:T(8,128)S(1)}, f32[32,16,32,64]{3,2,1,0:T(8,128)S(1)}, f32[512,512]{1,0:T(8,128)S(1)}, f32[256,512]{1,0:T(8,128)S(1)}, f32[512,128]{1,0:T(8,128)S(1)}) custom-call(f32[8,4,16,32,64]{4,3,2,1,0:T(8,128)} %bitcast.6, f32[8,4,16,32,64]{4,3,2,1,0:T(8,128)} %bitcast.7, f32[16,32,64]{2,1,0:T(8,128)} %refs_2_.1, ...), custom_call_target="tpu_custom_call" | custom-call | tf_op jit(solution)/shard_map/dft3/pallas_call | solution.py:308
  100.8 5.8 %put.1 = (f32[32,16,32,64]{3,2,1,0:T(8,128)}, f32[32,16,32,64]{3,2,1,0:T(8,128)}) custom-call(f32[32,16,32,64]{3,2,1,0:T(8,128)S(1)} %get-tuple-element.7.vr, f32[32,16,32,64]{3,2,1,0:T(8,128)S(1)} %get-tuple-element.8.vi, f32[512,512]{1,0:T(8,128)S(1)} %get-tuple-element.9.mat, f32[256,512]{1,0:T(8,128)S(1)} %get-tuple-element.10.last, ...), custom_call_target="tpu_custom_call" | custom-call | tf_op jit(solution)/shard_map/put/pallas_call | solution.py:329

commit v19 on v18

--- a/solution.py
+++ b/solution.py
@@ -107,7 +107,7 @@
         src, dst = (ur, ui)[k], inp.at[k]
         return pltpu.make_async_copy(src.at[g], dst.at[lax.rem(g, RING)], in_sem.at[lax.rem(g, RING)])
 
-    pieces = ((0, 2), (2, 2), (4, 4), (8, 8))
+    pieces = ((0, 2), (2, 2), (4, 4), (8, 4), (12, 4))
 
     def piece(i, k):
         src, dst = (ur, ui)[k], inp.at[k]
@@ -130,7 +130,7 @@
     for p in (1, 2, 3):
         pl.semaphore_signal(barrier, inc=1, device_id={"row": lax.rem(row + p, 4)}, device_id_type=MESH)
     pl.semaphore_signal(barrier, inc=1, device_id={"col": other}, device_id_type=MESH)
-    for i in range(1, 4):
+    for i in range(1, len(pieces)):
         start_piece(i)
 
     def step_x(g, first, count):
@@ -206,10 +206,8 @@
         if i == 0:
             pl.semaphore_wait(barrier, 4)
         send_row(0, 1, first, count).start()
-        if i == 1:
-            send_row(1, 1, 0, first + count).start()
     send_row(0, 0).start()
-    send_row(1, 1, 4, 12).start()
+    send_row(1, 1).start()
     send_row(1, 0).start()
     send_row(0, 2).start()
 
@@ -282,7 +280,7 @@
 
 def kernel(*refs):
     dma = pltpu.SemaphoreType.DMA
-    pl.run_scoped(functools.partial(body, *refs), in_sem=dma((RING,)), q_sem=dma((4,)), c_sem=dma((3,)), s1=dma,
+    pl.run_scoped(functools.partial(body, *refs), in_sem=dma((RING,)), q_sem=dma((5,)), c_sem=dma((3,)), s1=dma,
                   d1=dma((UNITS,)), s2=dma, d2=dma((UNITS // 2,)))
 
 

time: 107 us -> 106 us (level)
  no operation moved by 1% of the time
where the time goes in v19:
time: 106 us
  Pallas kernels  106 us (100%)
    pallas_call x1, Pallas kernels, local_forward(): pl.pallas_call(kernel, out_shape=[pltpu.VMEM((32, 16, 32, 64), f32)] * 2...  99.9 us
    pallas_call x1, Pallas kernels, local_forward(): pl.pallas_call(put, out_shape=[jax.ShapeDtypeStruct((32, 16, 32, 64), f32...  5.84 us

profile of v19, /device:TPU:1, one launch (start us, length us, event | category | flops | bytes accessed | tf_op | source)
XLA Modules:
  0.0 106.4 jit_solution(3491675517784959098)
XLA Ops:
  0.6 99.9 %dft3.1 = (f32[32,16,32,64]{3,2,1,0:T(8,128)S(1)}, f32[32,16,32,64]{3,2,1,0:T(8,128)S(1)}, f32[512,512]{1,0:T(8,128)S(1)}, f32[256,512]{1,0:T(8,128)S(1)}, f32[512,128]{1,0:T(8,128)S(1)}) custom-call(f32[8,4,16,32,64]{4,3,2,1,0:T(8,128)} %bitcast.6, f32[8,4,16,32,64]{4,3,2,1,0:T(8,128)} %bitcast.7, f32[16,32,64]{2,1,0:T(8,128)} %refs_2_.1, ...), custom_call_target="tpu_custom_call" | custom-call | tf_op jit(solution)/shard_map/dft3/pallas_call | solution.py:306
  100.5 5.8 %put.1 = (f32[32,16,32,64]{3,2,1,0:T(8,128)}, f32[32,16,32,64]{3,2,1,0:T(8,128)}) custom-call(f32[32,16,32,64]{3,2,1,0:T(8,128)S(1)} %get-tuple-element.7.vr, f32[32,16,32,64]{3,2,1,0:T(8,128)S(1)} %get-tuple-element.8.vi, f32[512,512]{1,0:T(8,128)S(1)} %get-tuple-element.9.mat, f32[256,512]{1,0:T(8,128)S(1)} %get-tuple-element.10.last, ...), custom_call_target="tpu_custom_call" | custom-call | tf_op jit(solution)/shard_map/put/pallas_call | solution.py:327

commit v20 on v19

--- a/solution.py
+++ b/solution.py
@@ -82,6 +82,12 @@
     return np.broadcast_to(both[..., None], (2, 8, 8, 128)).astype(np.float32)
 
 
+def gather(dst, lane, plane):
+    for kx in range(8):
+        for q in range(2):
+            dst[pl.ds(32 * kx, 32), pl.ds(lane + 128 * q, 128)] = plane(kx // 4, pl.ds(4 * q + kx % 4, 32, stride=8))
+
+
 def lane_product(lhs, mat, gain, outr, outi, at):
     for n in range(2):
         w = jnp.dot(lhs[...], mat[:, 256 * n : 256 * n + 256], precision=lax.Precision.HIGHEST,
@@ -92,7 +98,7 @@
             outi[at(2 * n + f)] = pair[:, 64:].reshape(8, 32, 64)
 
 
-def body(ur, ui, gf, wz, tw, outr, outi, wv, last, gv, inp, xbuf, b2, r2, tv, gs, asc, bsc, lsc,
+def body(ur, ui, gf, wz, tw, outr, outi, wv, own, got, gv, inp, xbuf, b2, r2, tv, gs, asc, bsc, lsc,
            in_sem, q_sem, c_sem, s1, d1, s2, d2):
     row, col = lax.axis_index("row"), lax.axis_index("col")
     core = lax.rem(row, 2)
@@ -165,9 +171,9 @@
             send_sem=s1, recv_sem=d1.at[u],
             device_id={"row": lax.rem(row + p, 4)}, device_id_type=MESH)
 
-    def send_col(u):
+    def send_col(u, dst):
         return pltpu.make_async_remote_copy(
-            src_ref=b2.at[u * 2 + other], dst_ref=r2.at[u],
+            src_ref=b2.at[u * 2 + other], dst_ref=dst,
             send_sem=s2, recv_sem=d2.at[u // 2], device_id={"col": other}, device_id_type=MESH)
 
     def step_y(u):
@@ -182,20 +188,19 @@
             b = packed_dft8([bsc[k1, y2] for y2 in range(8)])
             for k2 in range(8):
                 b2[u * 2 + k2 // 4, pl.ds(8 * (k1 + 8 * (k2 % 4)), 8), :] = b[k2]
-        send_col(u).start()
-
-    def gather_z(m, dst):
-        def part(lane, plane):
-            for kx in range(8):
-                for q in range(2):
-                    dst[pl.ds(32 * kx, 32), pl.ds(lane + 128 * q, 128)] = plane(2 * m + kx // 4, pl.ds(4 * q + kx % 4, 32, stride=8))
-
-        part(0, lambda u, rows: b2[u * 2 + col, rows, :])
+
+        @pl.when(u < UNITS - 2)
+        def _():
+            send_col(u, r2.at[u]).start()
+
+        @pl.when(u >= UNITS - 2)
+        def _():
+            send_col(u, got.at[u - UNITS + 2]).start()
+
+    def step_z(m):
+        gather(lsc, 0, lambda v, rows: b2[(2 * m + v) * 2 + col, rows, :])
         arrived(r2.at[pl.ds(2 * m, 2)], d2.at[m])
-        part(256, lambda u, rows: r2[u, rows, :])
-
-    def step_z(m):
-        gather_z(m, lsc)
+        gather(lsc, 256, lambda v, rows: r2[2 * m + v, rows, :])
         gain = gv[pl.ds(pl.multiple_of(256 * lax.rem(m, 2), 256), 256), :]
         lane_product(lsc, wv, gain, outr, outi, lambda f: (PACK * (m // 2) + f, pl.ds(8 * lax.rem(m, 2), 8)))
 
@@ -274,7 +279,9 @@
             step_z((t - LAG) // 2)
 
     arrived(xbuf.at[pl.ds(0, 3 * UNITS)], s1)
-    gather_z(UNITS // 2 - 1, last)
+    for v in range(2):
+        own[v] = b2[2 * (UNITS - 2 + v) + col]
+    arrived(got, d2.at[UNITS // 2 - 1])
     arrived(b2.at[pl.ds(0, UNITS)], s2)
 
 
@@ -284,12 +291,14 @@
                   d1=dma((UNITS,)), s2=dma, d2=dma((UNITS // 2,)))
 
 
-def put(vr, vi, mat, last, gain, outr, outi, lr, li, sem):
+def put(vr, vi, mat, own, got, gain, outr, outi, lr, li, lhs, sem):
     cuts = [(pl.ds(7 * i, 7), slice(None)) for i in range(4)] + [(pl.ds(28, 4), pl.ds(0, 8))]
     copies = [pltpu.make_async_copy(v.at[cut], o.at[cut], sem) for cut in cuts for v, o in ((vr, outr), (vi, outi))]
     for copy in copies:
         copy.start()
-    lane_product(last, mat, gain[256:, :], lr, li, lambda f: f)
+    gather(lhs, 0, lambda v, rows: own[v, rows, :])
+    gather(lhs, 256, lambda v, rows: got[v, rows, :])
+    lane_product(lhs, mat, gain[256:, :], lr, li, lambda f: f)
     cut = (pl.ds(28, 4), pl.ds(8, 8))
     tail = [pltpu.make_async_copy(v, o.at[cut], sem) for v, o in ((lr, outr), (li, outi))]
     for copy in tail:
@@ -306,9 +315,10 @@
         spectrum = pl.pallas_call(
             kernel,
             out_shape=[pltpu.VMEM((32, 16, 32, 64), f32)] * 2 + [
-                pltpu.VMEM((512, 512), f32), pltpu.VMEM((256, 512), f32), pltpu.VMEM((512, 128), f32)],
+                pltpu.VMEM((512, 512), f32), pltpu.VMEM((2, 256, 128), f32), pltpu.VMEM((2, 256, 128), f32),
+                pltpu.VMEM((512, 128), f32)],
             in_specs=[pl.BlockSpec(memory_space=pltpu.HBM)] * 5,
-            out_specs=[pl.BlockSpec(memory_space=pltpu.VMEM)] * 5,
+            out_specs=[pl.BlockSpec(memory_space=pltpu.VMEM)] * 6,
             scratch_shapes=[
                 pltpu.VMEM((2, RING, PACK, 16, 32, 64), f32),
                 pltpu.VMEM((UNITS * 7, 16, 8, 128), f32),
@@ -327,9 +337,9 @@
         return pl.pallas_call(
             put,
             out_shape=[jax.ShapeDtypeStruct((32, 16, 32, 64), f32)] * 2,
-            in_specs=[pl.BlockSpec(memory_space=pltpu.VMEM)] * 5,
+            in_specs=[pl.BlockSpec(memory_space=pltpu.VMEM)] * 6,
             out_specs=[pl.BlockSpec(memory_space=pltpu.HBM)] * 2,
-            scratch_shapes=[pltpu.VMEM((PACK, 8, 32, 64), f32)] * 2 + [pltpu.SemaphoreType.DMA],
+            scratch_shapes=[pltpu.VMEM((PACK, 8, 32, 64), f32)] * 2 + [pltpu.VMEM((256, 512), f32), pltpu.SemaphoreType.DMA],
             compiler_params=pltpu.CompilerParams(vmem_limit_bytes=8 * 1024 * 1024),
             name="put",
         )(*spectrum)

time: 106 us -> 106 us (level)
  no operation moved by 1% of the time
where the time goes in v20:
time: 106 us
  Pallas kernels  106 us (100%)
    pallas_call x1, Pallas kernels, local_forward(): pl.pallas_call(kernel, out_shape=[pltpu.VMEM((32, 16, 32, 64), f32)] * 2...  99.9 us
    pallas_call x1, Pallas kernels, local_forward(): pl.pallas_call(put, out_shape=[jax.ShapeDtypeStruct((32, 16, 32, 64), f32...  5.84 us

profile of v20, /device:TPU:1, one launch (start us, length us, event | category | flops | bytes accessed | tf_op | source)
XLA Modules:
  0.0 106.3 jit_solution(2095801045200037498)
XLA Ops:
  0.6 99.9 %dft3.1 = (f32[32,16,32,64]{3,2,1,0:T(8,128)S(1)}, f32[32,16,32,64]{3,2,1,0:T(8,128)S(1)}, f32[512,512]{1,0:T(8,128)S(1)}, f32[2,256,128]{2,1,0:T(8,128)S(1)}, f...) custom-call(f32[8,4,16,32,64]{4,3,2,1,0:T(8,128)} %bitcast.6, f32[8,4,16,32,64]{4,3,2,1,0:T(8,128)} %bitcast.7, ...), custom_call_target="tpu_custom_call" | custom-call | tf_op jit(solution)/shard_map/dft3/pallas_call | solution.py:315
  100.5 5.8 %put.1 = (f32[32,16,32,64]{3,2,1,0:T(8,128)}, f32[32,16,32,64]{3,2,1,0:T(8,128)}) custom-call(f32[32,16,32,64]{3,2,1,0:T(8,128)S(1)} %get-tuple-element.8.vr, f32[32,16,32,64]{3,2,1,0:T(8,128)S(1)} %get-tuple-element.9.vi, f32[512,512]{1,0:T(8,128)S(1)} %get-tuple-element.10.mat, f32[2,256,128]{2,1,0:T(8,128)S(1)} %get-tuple-element.11.own, ...), custom_call_target="tpu_custom_call" | custom-call | tf_op jit(solution)/shard_map/put/pallas_call | solution.py:337

commit v21 on v20

--- a/solution.py
+++ b/solution.py
@@ -113,11 +113,9 @@
         src, dst = (ur, ui)[k], inp.at[k]
         return pltpu.make_async_copy(src.at[g], dst.at[lax.rem(g, RING)], in_sem.at[lax.rem(g, RING)])
 
-    pieces = ((0, 2), (2, 2), (4, 4), (8, 4), (12, 4))
-
     def piece(i, k):
         src, dst = (ur, ui)[k], inp.at[k]
-        part = (0, slice(None), pl.ds(*pieces[i]))
+        part = (0, slice(None), pl.ds(2 * i, 2))
         return pltpu.make_async_copy(src.at[part], dst.at[part], q_sem.at[i])
 
     consts = [
@@ -136,8 +134,11 @@
     for p in (1, 2, 3):
         pl.semaphore_signal(barrier, inc=1, device_id={"row": lax.rem(row + p, 4)}, device_id_type=MESH)
     pl.semaphore_signal(barrier, inc=1, device_id={"col": other}, device_id_type=MESH)
-    for i in range(1, len(pieces)):
+
+    @pl.loop(1, 8)
+    def _(i):
         start_piece(i)
+
 
     def step_x(g, first, count):
         ring = lax.rem(g, RING)
@@ -159,10 +160,11 @@
                 xbuf[at, y] = jnp.where(top, vr, pltpu.roll(vi, 4, 0))
                 xbuf[at + 7, y] = jnp.where(top, pltpu.roll(vr, 4, 0), vi)
 
-        @pl.loop(0, count // 2)
-        def _(i):
+        def pair(i):
             one(i, 0)
             one(i, 1)
+
+        pl.loop(0, count // 2)(pair) if count > 2 else pair(0)
 
     def send_row(u, j, first=0, count=16):
         p = dests[j]
@@ -205,12 +207,19 @@
         lane_product(lsc, wv, gain, outr, outi, lambda f: (PACK * (m // 2) + f, pl.ds(8 * lax.rem(m, 2), 8)))
 
     consts[0].wait()
-    for i, (first, count) in enumerate(pieces):
-        arrived(inp.at[:, 0, :, pl.ds(first, count)], q_sem.at[i])
-        step_x(0, first, count)
-        if i == 0:
-            pl.semaphore_wait(barrier, 4)
-        send_row(0, 1, first, count).start()
+    def first_group(i):
+        arrived(inp.at[:, 0, :, pl.ds(2 * i, 2)], q_sem.at[i])
+        step_x(0, 2 * i, 2)
+
+    first_group(0)
+    pl.semaphore_wait(barrier, 4)
+    send_row(0, 1, 0, 2).start()
+
+    @pl.loop(1, 8)
+    def _(i):
+        first_group(i)
+        send_row(0, 1, 2 * i, 2).start()
+
     send_row(0, 0).start()
     send_row(1, 1).start()
     send_row(1, 0).start()
@@ -287,7 +296,7 @@
 
 def kernel(*refs):
     dma = pltpu.SemaphoreType.DMA
-    pl.run_scoped(functools.partial(body, *refs), in_sem=dma((RING,)), q_sem=dma((5,)), c_sem=dma((3,)), s1=dma,
+    pl.run_scoped(functools.partial(body, *refs), in_sem=dma((RING,)), q_sem=dma((8,)), c_sem=dma((3,)), s1=dma,
                   d1=dma((UNITS,)), s2=dma, d2=dma((UNITS // 2,)))
 
 

time: 106 us -> 106 us (level)
  no operation moved by 1% of the time
where the time goes in v21:
time: 106 us
  Pallas kernels  106 us (100%)
    pallas_call x1, Pallas kernels, local_forward(): pl.pallas_call(kernel, out_shape=[pltpu.VMEM((32, 16, 32, 64), f32)] * 2...  99.7 us
    pallas_call x1, Pallas kernels, local_forward(): pl.pallas_call(put, out_shape=[jax.ShapeDtypeStruct((32, 16, 32, 64), f32...  5.84 us

profile of v21, /device:TPU:1, one launch (start us, length us, event | category | flops | bytes accessed | tf_op | source)
XLA Modules:
  0.0 106.2 jit_solution(11751499372424247533)
XLA Ops:
  0.6 99.7 %dft3.1 = (f32[32,16,32,64]{3,2,1,0:T(8,128)S(1)}, f32[32,16,32,64]{3,2,1,0:T(8,128)S(1)}, f32[512,512]{1,0:T(8,128)S(1)}, f32[2,256,128]{2,1,0:T(8,128)S(1)}, f...) custom-call(f32[8,4,16,32,64]{4,3,2,1,0:T(8,128)} %bitcast.6, f32[8,4,16,32,64]{4,3,2,1,0:T(8,128)} %bitcast.7, ...), custom_call_target="tpu_custom_call" | custom-call | tf_op jit(solution)/shard_map/dft3/pallas_call | solution.py:324
  100.3 5.8 %put.1 = (f32[32,16,32,64]{3,2,1,0:T(8,128)}, f32[32,16,32,64]{3,2,1,0:T(8,128)}) custom-call(f32[32,16,32,64]{3,2,1,0:T(8,128)S(1)} %get-tuple-element.8.vr, f32[32,16,32,64]{3,2,1,0:T(8,128)S(1)} %get-tuple-element.9.vi, f32[512,512]{1,0:T(8,128)S(1)} %get-tuple-element.10.mat, f32[2,256,128]{2,1,0:T(8,128)S(1)} %get-tuple-element.11.own, ...), custom_call_target="tpu_custom_call" | custom-call | tf_op jit(solution)/shard_map/put/pallas_call | solution.py:346

commit v22 on v21

--- a/solution.py
+++ b/solution.py
@@ -11,7 +11,7 @@
 
 MESH = pl.DeviceIdType.MESH
 HALF = math.sqrt(0.5)
-GROUPS, PACK, UNITS, RING, LAG = 8, 4, 32, 4, 5
+GROUPS, PACK, UNITS, RING, LAG, BEHIND = 8, 4, 32, 4, 5, 2
 
 
 def interleave(even, odd):
@@ -213,12 +213,26 @@
 
     first_group(0)
     pl.semaphore_wait(barrier, 4)
-    send_row(0, 1, 0, 2).start()
+
+    @pl.when(core == 0)
+    def _():
+        send_row(0, 1, 0, 2).start()
 
     @pl.loop(1, 8)
     def _(i):
         first_group(i)
-        send_row(0, 1, 2 * i, 2).start()
+
+        @pl.when(core == 0)
+        def _():
+            send_row(0, 1, 2 * i, 2).start()
+
+        @pl.when((core == 1) & (i >= BEHIND))
+        def _():
+            send_row(0, 1, 2 * (i - BEHIND), 2).start()
+
+    @pl.when(core == 1)
+    def _():
+        send_row(0, 1, 16 - 2 * BEHIND, 2 * BEHIND).start()
 
     send_row(0, 0).start()
     send_row(1, 1).start()

time: 106 us -> 106 us (level)
  no operation moved by 1% of the time
where the time goes in v22:
time: 106 us
  Pallas kernels  106 us (100%)
    pallas_call x1, Pallas kernels, local_forward(): pl.pallas_call(kernel, out_shape=[pltpu.VMEM((32, 16, 32, 64), f32)] * 2...  99.7 us
    pallas_call x1, Pallas kernels, local_forward(): pl.pallas_call(put, out_shape=[jax.ShapeDtypeStruct((32, 16, 32, 64), f32...  5.84 us

profile of v22, /device:TPU:1, one launch (start us, length us, event | category | flops | bytes accessed | tf_op | source)
XLA Modules:
  0.0 106.2 jit_solution(2943476216914586215)
XLA Ops:
  0.6 99.7 %dft3.1 = (f32[32,16,32,64]{3,2,1,0:T(8,128)S(1)}, f32[32,16,32,64]{3,2,1,0:T(8,128)S(1)}, f32[512,512]{1,0:T(8,128)S(1)}, f32[2,256,128]{2,1,0:T(8,128)S(1)}, f...) custom-call(f32[8,4,16,32,64]{4,3,2,1,0:T(8,128)} %bitcast.6, f32[8,4,16,32,64]{4,3,2,1,0:T(8,128)} %bitcast.7, ...), custom_call_target="tpu_custom_call" | custom-call | tf_op jit(solution)/shard_map/dft3/pallas_call | solution.py:338
  100.3 5.8 %put.1 = (f32[32,16,32,64]{3,2,1,0:T(8,128)}, f32[32,16,32,64]{3,2,1,0:T(8,128)}) custom-call(f32[32,16,32,64]{3,2,1,0:T(8,128)S(1)} %get-tuple-element.8.vr, f32[32,16,32,64]{3,2,1,0:T(8,128)S(1)} %get-tuple-element.9.vi, f32[512,512]{1,0:T(8,128)S(1)} %get-tuple-element.10.mat, f32[2,256,128]{2,1,0:T(8,128)S(1)} %get-tuple-element.11.own, ...), custom_call_target="tpu_custom_call" | custom-call | tf_op jit(solution)/shard_map/put/pallas_call | solution.py:360

commit v23 on v22

--- a/solution.py
+++ b/solution.py
@@ -235,6 +235,11 @@
         send_row(0, 1, 16 - 2 * BEHIND, 2 * BEHIND).start()
 
     send_row(0, 0).start()
+
+    @pl.when(core == 1)
+    def _():
+        pl.delay(500)
+
     send_row(1, 1).start()
     send_row(1, 0).start()
     send_row(0, 2).start()

time: 106 us -> 106 us (level)
  no operation moved by 1% of the time
where the time goes in v23:
time: 106 us
  Pallas kernels  106 us (100%)
    pallas_call x1, Pallas kernels, local_forward(): pl.pallas_call(kernel, out_shape=[pltpu.VMEM((32, 16, 32, 64), f32)] * 2...  99.7 us
    pallas_call x1, Pallas kernels, local_forward(): pl.pallas_call(put, out_shape=[jax.ShapeDtypeStruct((32, 16, 32, 64), f32...  5.84 us

profile of v23, /device:TPU:1, one launch (start us, length us, event | category | flops | bytes accessed | tf_op | source)
XLA Modules:
  0.0 106.2 jit_solution(7516278421958997427)
XLA Ops:
  0.6 99.7 %dft3.1 = (f32[32,16,32,64]{3,2,1,0:T(8,128)S(1)}, f32[32,16,32,64]{3,2,1,0:T(8,128)S(1)}, f32[512,512]{1,0:T(8,128)S(1)}, f32[2,256,128]{2,1,0:T(8,128)S(1)}, f...) custom-call(f32[8,4,16,32,64]{4,3,2,1,0:T(8,128)} %bitcast.6, f32[8,4,16,32,64]{4,3,2,1,0:T(8,128)} %bitcast.7, ...), custom_call_target="tpu_custom_call" | custom-call | tf_op jit(solution)/shard_map/dft3/pallas_call | solution.py:343
  100.3 5.8 %put.1 = (f32[32,16,32,64]{3,2,1,0:T(8,128)}, f32[32,16,32,64]{3,2,1,0:T(8,128)}) custom-call(f32[32,16,32,64]{3,2,1,0:T(8,128)S(1)} %get-tuple-element.8.vr, f32[32,16,32,64]{3,2,1,0:T(8,128)S(1)} %get-tuple-element.9.vi, f32[512,512]{1,0:T(8,128)S(1)} %get-tuple-element.10.mat, f32[2,256,128]{2,1,0:T(8,128)S(1)} %get-tuple-element.11.own, ...), custom_call_target="tpu_custom_call" | custom-call | tf_op jit(solution)/shard_map/put/pallas_call | solution.py:365

commit v24 on v21

--- a/solution.py
+++ b/solution.py
@@ -11,7 +11,7 @@
 
 MESH = pl.DeviceIdType.MESH
 HALF = math.sqrt(0.5)
-GROUPS, PACK, UNITS, RING, LAG = 8, 4, 32, 4, 5
+GROUPS, PACK, UNITS, RING, LAG = 8, 4, 32, 4, 3
 
 
 def interleave(even, odd):

time: 106 us -> 106 us (level)
  no operation moved by 1% of the time
where the time goes in v24:
time: 106 us
  Pallas kernels  106 us (100%)
    pallas_call x1, Pallas kernels, local_forward(): pl.pallas_call(kernel, out_shape=[pltpu.VMEM((32, 16, 32, 64), f32)] * 2...  99.7 us
    pallas_call x1, Pallas kernels, local_forward(): pl.pallas_call(put, out_shape=[jax.ShapeDtypeStruct((32, 16, 32, 64), f32...  5.84 us

profile of v24, /device:TPU:1, one launch (start us, length us, event | category | flops | bytes accessed | tf_op | source)
XLA Modules:
  0.0 106.2 jit_solution(15287263863119530539)
XLA Ops:
  0.6 99.7 %dft3.1 = (f32[32,16,32,64]{3,2,1,0:T(8,128)S(1)}, f32[32,16,32,64]{3,2,1,0:T(8,128)S(1)}, f32[512,512]{1,0:T(8,128)S(1)}, f32[2,256,128]{2,1,0:T(8,128)S(1)}, f...) custom-call(f32[8,4,16,32,64]{4,3,2,1,0:T(8,128)} %bitcast.6, f32[8,4,16,32,64]{4,3,2,1,0:T(8,128)} %bitcast.7, ...), custom_call_target="tpu_custom_call" | custom-call | tf_op jit(solution)/shard_map/dft3/pallas_call | solution.py:324
  100.3 5.8 %put.1 = (f32[32,16,32,64]{3,2,1,0:T(8,128)}, f32[32,16,32,64]{3,2,1,0:T(8,128)}) custom-call(f32[32,16,32,64]{3,2,1,0:T(8,128)S(1)} %get-tuple-element.8.vr, f32[32,16,32,64]{3,2,1,0:T(8,128)S(1)} %get-tuple-element.9.vi, f32[512,512]{1,0:T(8,128)S(1)} %get-tuple-element.10.mat, f32[2,256,128]{2,1,0:T(8,128)S(1)} %get-tuple-element.11.own, ...), custom_call_target="tpu_custom_call" | custom-call | tf_op jit(solution)/shard_map/put/pallas_call | solution.py:346

commit v25 on v21

--- a/solution.py
+++ b/solution.py
@@ -131,9 +131,9 @@
     consts[0].start()
     start_piece(0)
     barrier = pltpu.get_barrier_semaphore()
-    for p in (1, 2, 3):
+    pl.semaphore_signal(barrier, inc=1, device_id={"col": other}, device_id_type=MESH)
+    for p in (dests[1], dests[2], dests[0]):
         pl.semaphore_signal(barrier, inc=1, device_id={"row": lax.rem(row + p, 4)}, device_id_type=MESH)
-    pl.semaphore_signal(barrier, inc=1, device_id={"col": other}, device_id_type=MESH)
 
     @pl.loop(1, 8)
     def _(i):

time: 106 us -> 106 us (level)
  no operation moved by 1% of the time
where the time goes in v25:
time: 106 us
  Pallas kernels  106 us (100%)
    pallas_call x1, Pallas kernels, local_forward(): pl.pallas_call(kernel, out_shape=[pltpu.VMEM((32, 16, 32, 64), f32)] * 2...  99.7 us
    pallas_call x1, Pallas kernels, local_forward(): pl.pallas_call(put, out_shape=[jax.ShapeDtypeStruct((32, 16, 32, 64), f32...  5.84 us

profile of v25, /device:TPU:1, one launch (start us, length us, event | category | flops | bytes accessed | tf_op | source)
XLA Modules:
  0.0 106.2 jit_solution(16589915254478351292)
XLA Ops:
  0.6 99.7 %dft3.1 = (f32[32,16,32,64]{3,2,1,0:T(8,128)S(1)}, f32[32,16,32,64]{3,2,1,0:T(8,128)S(1)}, f32[512,512]{1,0:T(8,128)S(1)}, f32[2,256,128]{2,1,0:T(8,128)S(1)}, f...) custom-call(f32[8,4,16,32,64]{4,3,2,1,0:T(8,128)} %bitcast.6, f32[8,4,16,32,64]{4,3,2,1,0:T(8,128)} %bitcast.7, ...), custom_call_target="tpu_custom_call" | custom-call | tf_op jit(solution)/shard_map/dft3/pallas_call | solution.py:324
  100.3 5.8 %put.1 = (f32[32,16,32,64]{3,2,1,0:T(8,128)}, f32[32,16,32,64]{3,2,1,0:T(8,128)}) custom-call(f32[32,16,32,64]{3,2,1,0:T(8,128)S(1)} %get-tuple-element.8.vr, f32[32,16,32,64]{3,2,1,0:T(8,128)S(1)} %get-tuple-element.9.vi, f32[512,512]{1,0:T(8,128)S(1)} %get-tuple-element.10.mat, f32[2,256,128]{2,1,0:T(8,128)S(1)} %get-tuple-element.11.own, ...), custom_call_target="tpu_custom_call" | custom-call | tf_op jit(solution)/shard_map/put/pallas_call | solution.py:346
